TPU v7x, 64 devices: a 2x2x8 block of a 4x4x8 slice. The times are simulated.
64 devices in a mesh: dp: 4 (over x, y), tp: 16 (over z, core).
Axes of the slice: x: 2, y: 2, z: 8, core: 2. Of those that a mesh axis runs over, the one named last changes fastest.
The devices are a block of a 4x4x8 slice.
Arguments:
- hidden: bfloat16 [64, 6, 4096], P('dp'), parts along dimension 0
- w_head: bfloat16 [4096, 128256], P(None, 'tp')
- q_draft: float32 [64, 5, 128256], P(('dp', 'tp')), parts along dimension 0
- x_draft: int32 [64, 5], P('dp'), parts along dimension 0
Outputs:
- output 1: float32 [64, 5], P(('dp', 'tp')), parts along dimension 0
- output 2: float32 [64], P(('dp', 'tp')), parts along dimension 0
- output 3: float32 [64, 5, 128256], P(('dp', 'tp')), parts along dimension 0
- output 4: float32 [64, 128256], P(('dp', 'tp')), parts along dimension 0
There are 4 independent parts. A program takes and returns all parts, laid end to end along the dimension named above; an argument that names none is the same for every part.
All inputs are finite; a program needn't handle non-finite values.
Results may differ from a plain program's by a relative error of at most 0.001.
Values are sent between devices in bfloat16 or wider.
A program may use at most 768 MiB of HBM per device.

v0:
```python
import jax
import jax.numpy as jnp
from jax import lax
from jax.sharding import PartitionSpec as P

INV_TEMP = 1.25


def verify_rows(logits, q_rows, x_rows):
    draft_len = q_rows.shape[1]
    row_peak = jnp.max(logits, axis=-1, keepdims=True)
    exp_vals = jnp.exp(logits - row_peak)
    target_p = exp_vals / jnp.sum(exp_vals, axis=-1, keepdims=True)
    draft_p = target_p[:, :draft_len]
    p_pick = jnp.take_along_axis(draft_p, x_rows[:, :, None], axis=2)[:, :, 0]
    q_pick = jnp.take_along_axis(q_rows, x_rows[:, :, None], axis=2)[:, :, 0]
    accept = jnp.minimum(1.0, p_pick / q_pick)
    expected = jnp.sum(jnp.cumprod(accept, axis=1), axis=1)
    excess = jnp.maximum(draft_p - q_rows, 0.0)
    residual = excess / jnp.sum(excess, axis=-1, keepdims=True)
    return accept, expected, residual, target_p[:, draft_len]


def solution(mesh):
    def local_step(hidden, w_shard, q_rows, x_group):
        seq_dev = q_rows.shape[0]
        logits = jnp.einsum("bjd,dv->bjv", hidden, w_shard, preferred_element_type=jnp.float32) * INV_TEMP
        seq_logits = lax.all_to_all(logits, "tp", 0, 2, tiled=True)
        tp_rank = lax.axis_index("tp")
        x_rows = lax.dynamic_slice_in_dim(x_group, tp_rank * seq_dev, seq_dev, axis=0)
        return verify_rows(seq_logits, q_rows, x_rows)

    return jax.shard_map(local_step, mesh=mesh,
                         in_specs=(P("dp", None, None), P(None, "tp"), P(("dp", "tp"), None, None), P("dp", None)),
                         out_specs=(P(("dp", "tp"), None), P(("dp", "tp")), P(("dp", "tp"), None, None), P(("dp", "tp"), None)),
                         check_vma=False)
```

profile of v0, /device:TPU:21, one launch (start us, length us, event | category | flops | bytes accessed | tf_op | source)
XLA Modules:
  0.0 173.5 jit_solution(5480594455769104590)
XLA Ops:
  0.6 0.0 copy-start
  0.6 1.1 copy-done
  1.8 28.9 %fusion.2 = f32[16,6,8016]{2,0,1:T(8,128)} fusion(bf16[16,6,4096]{2,0,1:T(8,128)(2,1)S(1)} %copy-done, bf16[4096,8016]{0,1:T(8,128)(2,1)} %param.7), kind=kOutput, calls=%fused_computation.4 | convolution fusion | flops 6304808448 | bytes 69531648 | tf_op jit(solution)/shard_map/bjd,dv->bjv/dot_general | solution.py:27
  30.7 4.8 %copy.12 = f32[16,6,8016]{2,1,0:T(8,128)} copy(f32[16,6,8016]{2,0,1:T(8,128)} %fusion.2) | data formatting | bytes 6156288 | tf_op jit(solution)/shard_map/mul | solution.py:27
  35.5 0.0 copy-start.4
  35.5 10.9 %all-to-all-start = ((f32[16,6,8016]{2,1,0:T(8,128)}), f32[16,6,8016]{2,1,0:T(8,128)}, u32[]{:S(2)}, u32[]{:S(2)}) async-start(f32[16,6,8016]{2,1,0:T(8,128)} %copy.12), calls=%async_computation | async-start | bytes 8257536 | tf_op jit(solution)/shard_map/all_to_all | solution.py:28
  46.4 0.0 copy-done.4
  46.4 0.2 dynamic-slice_reduce_fusion
  46.6 91.1 %all-to-all-done = f32[16,6,8016]{2,1,0:T(8,128)} async-done(((f32[16,6,8016]{2,1,0:T(8,128)}), f32[16,6,8016]{2,1,0:T(8,128)}, u32[]{:S(2)}, u32[]{:S(2)}) %all-to-all-start) | async-done | bytes 3078176 | tf_op jit(solution)/shard_map/all_to_all | solution.py:28
  137.8 4.5 %copy.13 = f32[1,6,16,8016]{3,2,0,1:T(8,128)} copy(f32[1,6,16,8016]{3,1,2,0:T(8,128)} %bitcast.2) | data formatting | bytes 6156288 | tf_op jit(solution)/shard_map/all_to_all | solution.py:28
  142.3 5.9 %all_to_all.17 = f32[1,6,128256]{2,1,0:T(8,128)} reshape(f32[1,6,16,8016]{3,2,0,1:T(8,128)} %copy.13) | data formatting | bytes 6156288 | tf_op jit(solution)/shard_map/all_to_all | solution.py:28
  148.2 3.3 %reduce_max.9 = f32[6]{0:T(128)S(1)} reduce(f32[16,6,8016]{2,1,0:T(8,128)} %all-to-all-done, f32[]{:T(128)} %constant.4.clone.1), dimensions={0,2}, to_apply=%region_0.0 | reduce | flops 769530 | bytes 3078172 | tf_op jit(solution)/shard_map/reduce_max | solution.py:11
  151.5 0.0 copy-start.2
  151.5 3.6 %exponential_reduce_fusion = f32[6]{0:T(128)S(1)} fusion(f32[6]{0:T(128)S(1)} %reduce_max.9, f32[16,6,8016]{2,1,0:T(8,128)} %all-to-all-done), kind=kLoop, calls=%fused_computation.7 | loop fusion | flops 1539066 | bytes 3078192 | tf_op jit(solution)/shard_map/reduce_sum | solution.py:13
  155.1 0.0 copy-done.2
  155.1 0.0 copy-start.3
  155.1 0.6 exponential_divide_fusion
  155.7 1.3 slice_bitcast_fusion.1
  157.0 0.0 copy-done.3
  157.0 1.5 fusion.6
  158.6 0.0 copy-start.1
  158.6 4.9 %broadcast_divide_fusion = (f32[1,5,128256]{2,1,0:T(8,128)}, f32[5,128256]{1,0:T(8,128)}, f32[5,128256]{1,0:T(8,128)}) fusion(f32[5]{0:T(128)S(1)} %fusion.6, f32[1,5,128256]{2,0,1:T(1,128)S(1)} %copy-done.3, f32[1,6,128256]{2,1,0:T(8,128)S(1)} %exponential_divide_fusion), kind=kLoop, calls=%fused_computation.11 | loop fusion | flops 1923840 | bytes 12825620 | tf_op jit(solution)/shard_map/div | solution.py:20
  163.5 1.5 gather_fusion
  164.9 1.5 gather_fusion.1
  166.4 6.3 %copy.16 = f32[1,5,128256]{2,0,1:T(1,128)} copy(f32[1,5,128256]{2,1,0:T(8,128)} %get-tuple-element.13) | data formatting | bytes 5130240
  172.7 0.0 copy-start.5
  172.7 0.2 reduce_window.9
  172.9 0.6 reduce_sum.30
  173.5 0.0 copy-done.5
  173.5 0.0 copy-done.1
  (5 shorter events, 0.0 us)
Async XLA Ops:
  0.6 1.1 copy-start
  35.5 10.9 %copy-start.4 = (s32[16,5]{0,1:T(8,128)S(1)}, s32[16,5]{0,1:T(8,128)}, u32[]{:S(2)}) copy-start(s32[16,5]{0,1:T(8,128)} %param.9) | copy-start | bytes 964
  35.5 102.2 %all-to-all-start = ((f32[16,6,8016]{2,1,0:T(8,128)}), f32[16,6,8016]{2,1,0:T(8,128)}, u32[]{:S(2)}, u32[]{:S(2)}) async-start(f32[16,6,8016]{2,1,0:T(8,128)} %copy.12), calls=%async_computation | async-start | bytes 8257536 | tf_op jit(solution)/shard_map/all_to_all | solution.py:28
  151.5 3.6 %copy-start.2 = (f32[1,6,128256]{2,1,0:T(8,128)S(1)}, f32[1,6,128256]{2,1,0:T(8,128)}, u32[]{:S(2)}) copy-start(f32[1,6,128256]{2,1,0:T(8,128)} %all_to_all.17) | copy-start | bytes 9234436
  155.1 1.9 %copy-start.3 = (f32[1,5,128256]{2,0,1:T(1,128)S(1)}, f32[1,5,128256]{2,0,1:T(1,128)}, u32[]{:S(2)}) copy-start(f32[1,5,128256]{2,0,1:T(1,128)} %param.8) | copy-start | bytes 7695364
  158.6 14.9 %copy-start.1 = (bf16[16,6,4096]{2,0,1:T(8,128)(2,1)S(1)}, bf16[16,6,4096]{2,0,1:T(8,128)(2,1)}, u32[]{:S(2)}) copy-start(bf16[16,6,4096]{2,0,1:T(8,128)(2,1)} %param.6) | copy-start | bytes 2359300
  172.7 0.8 copy-start.5
where the time goes:
time: 174 us; the launch traced here: 173 us
  waiting for transfers between devices  91.1 us (52%)
  matrix products  28.9 us (17%)
  local copies, waits for them, and re-layouts  27.1 us (16%)
  other arithmetic  14.8 us (9%)
  starting transfers between devices  10.9 us (6%)
    all_to_all x1, waiting for transfers between devices, local_step(): seq_logits = lax.all_to_all(logits, 'tp', 0, 2, tiled=True)  91.1 us
    dot_general x1, matrix products, local_step(): jnp.einsum('bjd,dv->bjv', hidden, w_shard, preferred_element_type=jnp.flo...  28.9 us
    all_to_all x1, starting transfers between devices, local_step(): seq_logits = lax.all_to_all(logits, 'tp', 0, 2, tiled=True)  10.9 us
    all_to_all x2, local copies, waits for them, and re-layouts, local_step(): seq_logits = lax.all_to_all(logits, 'tp', 0, 2, tiled=True)  10.4 us
    unnamed x13, local copies, waits for them, and re-layouts  7.43 us
    div x1, other arithmetic, verify_rows(): residual = excess / jnp.sum(excess, axis=-1, keepdims=True)  4.9 us
    mul x1, local copies, waits for them, and re-layouts, local_step(): jnp.einsum('bjd,dv->bjv', hidden, w_shard, preferred_element_type=jnp.flo...  4.81 us
    reduce_sum x1, other arithmetic, verify_rows(): target_p = exp_vals / jnp.sum(exp_vals, axis=-1, keepdims=True)  3.57 us
  transfers between devices with their start and end apart: 1, of which 1 were waited for; matrix products, arithmetic and copies ran while one was open for 0% of the time, Pallas kernels for 0%

commit v1 on v0

v1 whole, which is shorter than its diff:
```python
import functools

import jax
import jax.numpy as jnp
from jax import lax
from jax.experimental import pallas as pl
from jax.experimental.pallas import tpu as pltpu
from jax.sharding import PartitionSpec as P

INV_TEMP = 1.25
LANES = 128
SUB = 8
TILE_ROWS = 2
NBUF = 4
AXIS = "tp"
MESH = pl.DeviceIdType.MESH


def exchange_kernel(geo, w_ref, h_ref, q_ref, x_ref, pe_ref, aux_ref, scale_ref,
                    hraw, hperm, ebuf, wbuf, send, recv, qbuf, stat_send, stat_recv, peak,
                    hsem, esem, wsem, qsem, ssem, rsem, tsem, usem):
    n, width, slots, pos_n, draft, batch, total_rows = geo
    f32 = jnp.float32
    me = lax.axis_index(AXIS)
    chip, core = me // 2, lax.rem(me, 2)
    chips = n // 2
    first_col = me * width
    off = pl.multiple_of(lax.rem(first_col, LANES), 16)
    last_fill = width - (slots - 1) * LANES
    slack = LANES - last_fill
    tail = pl.multiple_of(jnp.maximum(off - slack, 0), 16)
    positions = draft + 1

    hcopy = pltpu.make_async_copy(h_ref, hraw, hsem)
    hcopy.start()
    e1 = pltpu.make_async_copy(w_ref.at[pl.ds(0, LANES)], ebuf.at[pl.ds(pl.multiple_of(LANES + off, 16), LANES)], esem.at[0])
    e2 = pltpu.make_async_copy(w_ref.at[pl.ds(width - LANES, LANES)], ebuf.at[pl.ds(tail, LANES)], esem.at[1])
    want = (slots - 2) * LANES - off
    src3 = pl.multiple_of(jnp.minimum(want, width - 2 * LANES), 16)
    dst3 = pl.multiple_of(3 * LANES + slack + (src3 - want), 16)
    e3 = pltpu.make_async_copy(w_ref.at[pl.ds(src3, 2 * LANES)], ebuf.at[pl.ds(dst3, 2 * LANES)], esem.at[2])
    e1.start()
    e2.start()
    e3.start()

    tile_cols = TILE_ROWS * LANES
    tiles = (slots - 3) // TILE_ROWS

    def w_copy(t):
        start = pl.multiple_of(LANES - off + t * tile_cols, 16)
        slot = lax.rem(t, NBUF)
        return pltpu.make_async_copy(w_ref.at[pl.ds(start, tile_cols)], wbuf.at[slot], wsem.at[slot])

    for t in range(NBUF - 1):
        w_copy(t).start()

    barrier = pltpu.get_barrier_semaphore()
    for k in range(1, n):
        pl.semaphore_signal(barrier, inc=1, device_id={AXIS: lax.rem(me + k, n)}, device_id_type=MESH)

    rows_in, rows_out = positions * batch, SUB * batch
    ri = lax.broadcasted_iota(jnp.int32, (rows_out, rows_in), 0)
    ci = lax.broadcasted_iota(jnp.int32, (rows_out, rows_in), 1)
    pick = ((lax.rem(ri, SUB) * batch + ri // SUB) == ci).astype(f32).astype(jnp.bfloat16)
    hcopy.wait()
    depth = hraw.shape[1]
    hstep = 512

    @pl.loop(0, depth // hstep)
    def _(k):
        cols = pl.ds(pl.multiple_of(k * hstep, hstep), hstep)
        hperm[:, cols] = jnp.dot(pick, hraw[:, cols], preferred_element_type=f32).astype(jnp.bfloat16)

    def logits_of(block):
        z = lax.dot_general(hperm[...], block, (((1,), (1,)), ((), ())), preferred_element_type=f32)
        return z * INV_TEMP

    def put(z, pos):
        z3 = z.reshape(batch, SUB, LANES)
        send[:, pos] = z3
        return z3

    lane_e = lax.broadcasted_iota(jnp.int32, (1, 1, LANES), 2)
    ok_first = jnp.logical_or(lane_e >= off, lane_e < tail)
    ok_last = lane_e < jnp.minimum(off + last_fill, LANES)
    low = jnp.finfo(jnp.float32).min
    e1.wait()
    e2.wait()
    e3.wait()
    z_a = put(logits_of(ebuf[pl.ds(LANES, LANES), :]), 0)
    z_bc = logits_of(ebuf[pl.ds(3 * LANES + slack, 2 * LANES), :])
    z_b = put(z_bc[:, :LANES], 1)
    z_c = put(z_bc[:, LANES:], 2)
    peak[...] = jnp.maximum(jnp.where(ok_first, z_a, low), jnp.maximum(z_b, jnp.where(ok_last, z_c, low)))

    order = []
    for d in range(chips // 2, 0, -1):
        order += [(d, 0), (d, 1)]
        if 2 * d != chips:
            order += [(chips - d, 0), (chips - d, 1)]
    order.append((0, 1))

    def targets():
        for dz, dc in order:
            yield lax.rem(chip + dz, chips) * 2 + lax.rem(core + dc, 2)

    def send_group(g, pos, size):
        for tgt in targets():
            pltpu.make_async_remote_copy(
                src_ref=send.at[tgt, pl.ds(pos, size), pl.ds(0, positions), :],
                dst_ref=recv.at[me, pl.ds(pos, size), pl.ds(0, positions), :],
                send_sem=ssem.at[g], recv_sem=rsem.at[g], device_id={AXIS: tgt}, device_id_type=MESH).start()

    def keep_own(pos, size):
        for i in range(size):
            recv[me, pos + i] = send[me, pos + i]

    keep_own(0, 3)
    pl.semaphore_wait(barrier, n - 1)
    send_group(0, 0, 3)

    big = 4
    head = tiles % big
    head_rows, big_rows = head * TILE_ROWS, big * TILE_ROWS
    n_big = tiles // big
    groups = 2 + n_big
    held = 2

    @pl.loop(0, tiles)
    def _(t):
        @pl.when(t + NBUF - 1 < tiles)
        def _():
            w_copy(t + NBUF - 1).start()

        w_copy(t).wait()
        z = logits_of(wbuf[lax.rem(t, NBUF)])
        top = peak[...]
        for i in range(TILE_ROWS):
            top = jnp.maximum(top, put(z[:, i * LANES:(i + 1) * LANES], 3 + t * TILE_ROWS + i))
        peak[...] = top
        keep_own(3 + t * TILE_ROWS, TILE_ROWS)

        @pl.when(t == head - 1)
        def _():
            send_group(1, 3, head_rows)

        done = (t + 1 - head) // big

        @pl.when(jnp.logical_and(t >= head, jnp.logical_and(lax.rem(t + 1 - head, big) == 0, done <= n_big - held)))
        def _():
            send_group(1 + done, 3 + head_rows + (done - 1) * big_rows, big_rows)

    for j in range(draft):
        pltpu.make_async_copy(q_ref.at[j, :, 0, :], qbuf.at[:, j, :], qsem.at[j]).start()

    lane8 = lax.broadcasted_iota(jnp.int32, (SUB, LANES), 1)
    sub8 = lax.broadcasted_iota(jnp.int32, (SUB, LANES), 0)
    diag_m = lane8 == sub8
    diag_l = lane8 == sub8 + SUB

    @pl.loop(0, batch)
    def _(b):
        m = jnp.max(peak[b], axis=1, keepdims=True)
        acc = (jnp.where(ok_first[0], jnp.exp(send[b, 0] - m), 0.0) + jnp.exp(send[b, 1] - m)
               + jnp.where(ok_last[0], jnp.exp(send[b, 2] - m), 0.0))
        accs = [acc, jnp.zeros_like(acc), jnp.zeros_like(acc), jnp.zeros_like(acc)]
        for r in range(3, slots):
            accs[r % 4] = accs[r % 4] + jnp.exp(send[b, r] - m)
        l = jnp.sum((accs[0] + accs[1]) + (accs[2] + accs[3]), axis=1, keepdims=True)
        row = jnp.where(diag_m, m, 0.0) + jnp.where(diag_l, l, 0.0)
        stat_send[b] = jnp.sum(row, axis=0, keepdims=True)

    stat_recv[me] = stat_send[me]
    for tgt in targets():
        pltpu.make_async_remote_copy(src_ref=stat_send.at[tgt], dst_ref=stat_recv.at[me], send_sem=tsem, recv_sem=usem,
                                     device_id={AXIS: tgt}, device_id_type=MESH).start()
    for g in range(groups - held, groups):
        send_group(g, 3 + head_rows + (g - 2) * big_rows, big_rows)

    others = n - 1
    pltpu.make_async_copy(stat_recv.at[pl.ds(0, others)], stat_recv.at[pl.ds(0, others)], usem).wait()
    stats = [stat_recv[s] for s in range(n)]
    top = functools.reduce(jnp.maximum, stats)
    tot = jnp.zeros_like(top)
    for s in range(n):
        tot = tot + jnp.exp(stats[s] - top) * pltpu.roll(stats[s], LANES - SUB, 1)

    def spread(row):
        return jnp.sum(jnp.where(diag_m, row, 0.0), axis=1, keepdims=True)

    peak_g = jnp.broadcast_to(spread(top), (SUB, LANES))
    inv_sum = jnp.broadcast_to(1.0 / spread(tot), (SUB, LANES))

    for j in range(draft):
        pltpu.make_async_copy(q_ref.at[j, :, 0, :], qbuf.at[:, j, :], qsem.at[j]).wait()

    is_draft = sub8 < draft

    def excess_of(z, row):
        p = jnp.exp(z - peak_g) * inv_sum
        e = jnp.maximum(p - jnp.where(is_draft, qbuf[row], 0.0), 0.0)
        pe_ref[pl.ds(pl.multiple_of(row * SUB, SUB), SUB), :] = e
        return e

    def wait_group(g, pos, size):
        view = recv.at[pl.ds(0, others), pl.ds(pos, size), pl.ds(0, positions), :]
        pltpu.make_async_copy(view, view, rsem.at[g]).wait()

    lane_s = lane8
    parts = {}
    for s in range(n):
        first, o = (s * width) // LANES, (s * width) % LANES
        t_s = max(o - slack, 0)
        parts.setdefault(first, []).append((s, 0, o, LANES))
        if t_s:
            parts.setdefault(first + slots, []).append((s, 0, 0, t_s))
        parts.setdefault(first + slots - 1, []).append((s, 2, 0, min(LANES, o + last_fill)))
        parts.setdefault(first + slots - 2, []).append((s, 1, 0, LANES))
    wait_group(0, 0, 3)
    acc = jnp.zeros((SUB, LANES), f32)
    for row, pieces in sorted(parts.items()):
        z = recv[pieces[0][0], pieces[0][1]]
        for s, pos, lo, hi in pieces[1:]:
            z = jnp.where(jnp.logical_and(lane_s >= lo, lane_s < hi), recv[s, pos], z)
        acc = acc + excess_of(z, row)

    def main_rows(pos, size, acc):
        def one(s, acc):
            base = (s * width) // LANES + pos - 2
            es = [excess_of(recv[s, pos + i], base + i) for i in range(size)]
            while len(es) > 1:
                es = [es[i] + es[i + 1] for i in range(0, len(es) - 1, 2)] + ([es[-1]] if len(es) % 2 else [])
            return acc + es[0]
        return lax.fori_loop(0, n, one, acc)

    wait_group(1, 3, head_rows)
    acc = main_rows(3, head_rows, acc)

    def one_group(g, acc):
        pos = 3 + head_rows + (g - 2) * big_rows
        wait_group(g, pos, big_rows)
        return main_rows(pos, big_rows, acc)

    acc = lax.fori_loop(2, groups, one_group, acc)
    scale_ref[...] = jnp.broadcast_to(jnp.where(sub8[:, :1] < draft, 1.0 / jnp.sum(acc, axis=1, keepdims=True), 1.0), (SUB, LANES))

    prod = jnp.ones((1, 1), f32)
    expect = jnp.zeros((1, 1), f32)
    lane1 = lax.broadcasted_iota(jnp.int32, (1, LANES), 1)
    out_row = jnp.zeros((1, LANES), f32)
    for j in range(draft):
        x = x_ref[j, me]
        s = x // width
        row = x // LANES
        slot = row - (s * width) // LANES
        slot = jnp.where(slot == slots, 0, slot)
        pos = jnp.where(slot == 0, 0, jnp.where(slot >= slots - 2, slot - (slots - 3), slot + 2))
        here = jnp.logical_and(sub8 == j, lane8 == lax.rem(x, LANES))
        p = jnp.exp(recv[s, pos] - peak_g) * inv_sum

        def at_token(v):
            return jnp.sum(jnp.sum(jnp.where(here, v, 0.0), axis=1, keepdims=True), axis=0, keepdims=True)

        ratio = jnp.minimum(1.0, at_token(p) / at_token(qbuf[row]))
        prod = prod * ratio
        expect = expect + prod
        out_row = jnp.where(lane1 == j, ratio, out_row)
    out_row = jnp.where(lane1 == draft, expect, out_row)
    aux_ref[...] = jnp.broadcast_to(out_row, (SUB, LANES))

    def wait_sent(g, pos, size):
        view = send.at[pl.ds(0, others), pl.ds(pos, size), pl.ds(0, positions), :]
        pltpu.make_async_copy(view, view, ssem.at[g]).wait()

    wait_sent(0, 0, 3)
    wait_sent(1, 3, head_rows)

    @pl.loop(2, groups)
    def _(g):
        wait_sent(g, 3 + head_rows + (g - 2) * big_rows, big_rows)

    pltpu.make_async_copy(stat_send.at[pl.ds(0, others)], stat_send.at[pl.ds(0, others)], tsem).wait()


def finish_kernel(geo, pe_ref, scale_ref, aux_ref, res_ref, bonus_ref, acc_ref, exp_ref, stage, sem):
    total_rows, padded, draft, cuts = geo
    acc_ref[...] = aux_ref[0:1, 0:draft]
    exp_ref[...] = aux_ref[0:1, draft:draft + 1]
    scales = [jnp.broadcast_to(scale_ref[j:j + 1, :], (SUB, LANES)) for j in range(draft)]
    copies = []
    for c, (lo, hi) in enumerate(cuts):
        @pl.loop(lo // SUB, -(-hi // SUB))
        def _(k):
            for j in range(draft + 1):
                v = pe_ref[pl.ds(k * SUB * SUB + j, SUB, stride=SUB), :]
                stage[j, pl.ds(pl.multiple_of(k * SUB, SUB), SUB), :] = v * scales[j] if j < draft else v
        for j in range(draft + 1):
            dst = res_ref.at[j, pl.ds(lo, hi - lo), 0, :] if j < draft else bonus_ref.at[pl.ds(lo, hi - lo), 0, :]
            copies.append(pltpu.make_async_copy(stage.at[j, pl.ds(lo, hi - lo), :], dst, sem.at[c, j]))
            copies[-1].start()
    for cp in copies:
        cp.wait()


def solution(mesh):
    n = mesh.shape[AXIS]

    def local_step(hidden, w_shard, q_rows, x_group):
        f32 = jnp.float32
        batch, positions, depth = hidden.shape
        draft = positions - 1
        width = w_shard.shape[1]
        vocab = q_rows.shape[2]
        slots = -(-width // LANES)
        total_rows = vocab // LANES
        padded = -(-total_rows // SUB) * SUB
        slack = LANES - (width - (slots - 1) * LANES)
        h = jnp.transpose(hidden, (1, 0, 2)).reshape(positions * batch, depth)
        w = jnp.transpose(w_shard)
        q = jnp.transpose(q_rows, (1, 0, 2)).reshape(draft, total_rows, 1, LANES)
        x = jnp.transpose(x_group)
        tiles = (slots - 3) // TILE_ROWS
        groups = 2 + tiles // 4
        hbm = pl.BlockSpec(memory_space=pltpu.HBM)
        vmem = pl.BlockSpec(memory_space=pltpu.VMEM)
        geo = (n, width, slots, slots, draft, batch, total_rows)
        pe, aux, scale = pl.pallas_call(
            functools.partial(exchange_kernel, geo),
            name="verify_exchange",
            out_shape=(jax.ShapeDtypeStruct((padded * SUB, LANES), f32),
                       jax.ShapeDtypeStruct((SUB, LANES), f32),
                       jax.ShapeDtypeStruct((SUB, LANES), f32)),
            in_specs=[hbm, hbm, hbm, pl.BlockSpec(memory_space=pltpu.SMEM)],
            out_specs=(vmem, vmem, vmem),
            scratch_shapes=[
                pltpu.VMEM((positions * batch, depth), jnp.bfloat16),
                pltpu.VMEM((SUB * batch, depth), jnp.bfloat16),
                pltpu.VMEM((5 * LANES + slack, depth), jnp.bfloat16),
                pltpu.VMEM((NBUF, TILE_ROWS * LANES, depth), jnp.bfloat16),
                pltpu.VMEM((batch, slots, SUB, LANES), f32),
                pltpu.VMEM((n, slots, SUB, LANES), f32),
                pltpu.VMEM((total_rows, SUB, LANES), f32),
                pltpu.VMEM((batch, 1, LANES), f32),
                pltpu.VMEM((n, 1, LANES), f32),
                pltpu.VMEM((batch, SUB, LANES), f32),
                pltpu.SemaphoreType.DMA,
                pltpu.SemaphoreType.DMA((3,)),
                pltpu.SemaphoreType.DMA((NBUF,)),
                pltpu.SemaphoreType.DMA((draft,)),
                pltpu.SemaphoreType.DMA((groups,)),
                pltpu.SemaphoreType.DMA((groups,)),
                pltpu.SemaphoreType.DMA,
                pltpu.SemaphoreType.DMA,
            ],
            compiler_params=pltpu.CompilerParams(collective_id=0, has_side_effects=True, vmem_limit_bytes=40 * 2**20),
        )(w, h, q, x)
        step = -(-padded // 8 // SUB) * SUB
        cuts = tuple((lo, min(lo + step, total_rows)) for lo in range(0, total_rows, step))
        res, bonus, accept, expected = pl.pallas_call(
            functools.partial(finish_kernel, (total_rows, padded, draft, cuts)),
            name="verify_finish",
            out_shape=(jax.ShapeDtypeStruct((draft, total_rows, 1, LANES), f32),
                       jax.ShapeDtypeStruct((total_rows, 1, LANES), f32),
                       jax.ShapeDtypeStruct((1, draft), f32),
                       jax.ShapeDtypeStruct((1, 1), f32)),
            in_specs=[vmem, vmem, vmem],
            out_specs=(hbm, hbm, vmem, vmem),
            scratch_shapes=[pltpu.VMEM((positions, padded, LANES), f32), pltpu.SemaphoreType.DMA((len(cuts), positions))],
        )(pe, scale, aux)
        residual = jnp.transpose(res.reshape(draft, 1, vocab), (1, 0, 2))
        return accept, expected.reshape(1), residual, bonus.reshape(1, vocab)

    return jax.shard_map(local_step, mesh=mesh,
                         in_specs=(P("dp", None, None), P(None, AXIS), P(("dp", AXIS), None, None), P("dp", None)),
                         out_specs=(P(("dp", AXIS), None), P(("dp", AXIS)), P(("dp", AXIS), None, None), P(("dp", AXIS), None)),
                         check_vma=False)
```

time: 174 us -> 93.9 us (0.54)
  waiting for transfers between devices: 91.1 us -> 0 us
  Pallas kernels: 0 us -> 86.5 us
  matrix products: 28.9 us -> 0 us
  local copies, waits for them, and re-layouts: 27.1 us -> 6.63 us
  other arithmetic: 14.8 us -> 0 us
  starting transfers between devices: 10.9 us -> 0 us
    all_to_all x1 -> x0, waiting for transfers between devices: 91.1 us -> none  [local_step(): seq_logits = lax.all_to_all(logits, 'tp', 0, 2, tiled=True)]
    pallas_call x0 -> x2, Pallas kernels: none -> 86.5 us  [the longest x1 81.3 us: local_step(): pl.pallas_call(functools.partial(exchange_kernel, geo), name='verify_exch...]
    dot_general x1 -> x0, matrix products: 28.9 us -> none  [local_step(): jnp.einsum('bjd,dv->bjv', hidden, w_shard, preferred_element_type=jnp.flo...]
    all_to_all x1 -> x0, starting transfers between devices: 10.9 us -> none  [local_step(): seq_logits = lax.all_to_all(logits, 'tp', 0, 2, tiled=True)]
    all_to_all x2 -> x0, local copies, waits for them, and re-layouts: 10.4 us -> none  [local_step(): seq_logits = lax.all_to_all(logits, 'tp', 0, 2, tiled=True)]
    reduce_sum x3 -> x0, other arithmetic: 5.72 us -> none  [the longest x1 3.57 us: verify_rows(): target_p = exp_vals / jnp.sum(exp_vals, axis=-1, keepdims=True)]
    div x2 -> x0, other arithmetic: 5.51 us -> none  [the longest x1 4.9 us: verify_rows(): residual = excess / jnp.sum(excess, axis=-1, keepdims=True)]
    mul x1 -> x0, local copies, waits for them, and re-layouts: 4.81 us -> none  [local_step(): jnp.einsum('bjd,dv->bjv', hidden, w_shard, preferred_element_type=jnp.flo...]
  transfers between devices with their start and end apart: 1 -> 0, of which waited for: 1 -> 0; matrix products, arithmetic and copies ran while one was open for 0% -> 0% of each run, Pallas kernels for 0% -> 0%
where the time goes in v1:
time: 93.9 us; the launch traced here: 93.8 us
  Pallas kernels  86.5 us (92%)
  local copies, waits for them, and re-layouts  6.63 us (7%)
    pallas_call x1, Pallas kernels, local_step(): pl.pallas_call(functools.partial(exchange_kernel, geo), name='verify_exch...  81.3 us
    unnamed x12, local copies, waits for them, and re-layouts  6.63 us
    pallas_call x1, Pallas kernels, local_step(): pl.pallas_call(functools.partial(finish_kernel, (total_rows, padded, draf...  5.17 us

profile of v1, /device:TPU:21, one launch (start us, length us, event | category | flops | bytes accessed | tf_op | source)
XLA Modules:
  0.0 93.8 jit_solution(17254664103754642571)
XLA Ops:
  0.6 0.0 copy-start.1
  0.6 1.7 %copy-done.1 = f32[1,5,128256]{2,0,1:T(1,128)S(1)} copy-done((f32[1,5,128256]{2,0,1:T(1,128)S(1)}, f32[1,5,128256]{2,0,1:T(1,128)}, u32[]{:S(2)}) %copy-start.1) | copy-done | bytes 2565144
  2.4 0.0 copy-start.2
  2.4 1.1 %copy-done.2 = bf16[16,6,4096]{2,0,1:T(8,128)(2,1)S(1)} copy-done((bf16[16,6,4096]{2,0,1:T(8,128)(2,1)S(1)}, bf16[16,6,4096]{2,0,1:T(8,128)(2,1)}, u32[]{:S(2)}) %copy-start.2) | copy-done | bytes 786456
  3.5 0.0 copy-start.3
  3.5 0.7 copy-done.3
  4.2 81.3 %verify_exchange.1 = (f32[8064,128]{1,0:T(8,128)S(1)}, f32[8,128]{1,0:T(8,128)S(1)}, f32[8,128]{1,0:T(8,128)S(1)}) custom-call(bf16[8016,4096]{1,0:T(8,128)(2,1)} %bitcast.12, bf16[96,4096]{1,0:T(8,128)(2,1)S(1)} %bitcast.10, f32[5,1002,1,128]{3,2,1,0:T(1,128)S(1)} %bitcast.9, s32[5,16]{1,0:T(8,128)S(1)} %bitcast.11), custom_call_target="tpu_custom_call" | custom-call | tf_op jit(solution)/shard_map/verify_exchange/pallas_call | solution.py:327
  85.5 0.0 copy-start
  85.5 1.9 %copy-done = f32[8064,128]{1,0:T(8,128)} copy-done((f32[8064,128]{1,0:T(8,128)}, f32[8064,128]{1,0:T(8,128)S(1)}, u32[]{:S(2)}) %copy-start) | copy-done | bytes 4128792
  87.4 0.0 copy-start.4
  87.4 0.6 copy-done.4
  88.0 0.0 copy-start.5
  88.0 0.6 copy-done.5
  88.6 5.2 %verify_finish.1 = (f32[5,1002,1,128]{3,2,1,0:T(1,128)}, f32[1002,1,128]{2,1,0:T(1,128)}, f32[1,5]{1,0:T(1,128)}, f32[1,1]{1,0:T(1,128)}) custom-call(f32[8064,128]{1,0:T(8,128)} %copy-done, f32[8,128]{1,0:T(8,128)} %copy-done.5, f32[8,128]{1,0:T(8,128)} %copy-done.4), custom_call_target="tpu_custom_call" | custom-call | tf_op jit(solution)/shard_map/verify_finish/pallas_call | solution.py:359
Async XLA Ops:
  0.6 1.7 %copy-start.1 = (f32[1,5,128256]{2,0,1:T(1,128)S(1)}, f32[1,5,128256]{2,0,1:T(1,128)}, u32[]{:S(2)}) copy-start(f32[1,5,128256]{2,0,1:T(1,128)} %param.6) | copy-start | bytes 7695364
  2.4 1.1 %copy-start.2 = (bf16[16,6,4096]{2,0,1:T(8,128)(2,1)S(1)}, bf16[16,6,4096]{2,0,1:T(8,128)(2,1)}, u32[]{:S(2)}) copy-start(bf16[16,6,4096]{2,0,1:T(8,128)(2,1)} %param.4) | copy-start | bytes 2359300
  3.5 0.7 copy-start.3
  85.5 1.9 %copy-start = (f32[8064,128]{1,0:T(8,128)}, f32[8064,128]{1,0:T(8,128)S(1)}, u32[]{:S(2)}) copy-start(f32[8064,128]{1,0:T(8,128)S(1)} %get-tuple-element.11.pe_ref) | copy-start | bytes 12386308
  87.4 0.6 copy-start.4
  88.0 0.6 copy-start.5

commit v2 on v1

--- a/solution.py
+++ b/solution.py
@@ -16,9 +16,9 @@
 MESH = pl.DeviceIdType.MESH
 
 
-def exchange_kernel(geo, w_ref, h_ref, q_ref, x_ref, pe_ref, aux_ref, scale_ref,
-                    hraw, hperm, ebuf, wbuf, send, recv, qbuf, stat_send, stat_recv, peak,
-                    hsem, esem, wsem, qsem, ssem, rsem, tsem, usem):
+def exchange_kernel(geo, w_ref, h_ref, q_ref, x_hbm, pe_ref,
+                    x_ref, hraw, hperm, ebuf, wbuf, send, recv, qbuf, stat_send, stat_recv, peak,
+                    xsem, hsem, esem, wsem, qsem, ssem, rsem, tsem, usem):
     n, width, slots, pos_n, draft, batch, total_rows = geo
     f32 = jnp.float32
     me = lax.axis_index(AXIS)
@@ -53,6 +53,8 @@
 
     for t in range(NBUF - 1):
         w_copy(t).start()
+    xcopy = pltpu.make_async_copy(x_hbm, x_ref, xsem)
+    xcopy.start()
 
     barrier = pltpu.get_barrier_semaphore()
     for k in range(1, n):
@@ -242,8 +244,9 @@
         return main_rows(pos, big_rows, acc)
 
     acc = lax.fori_loop(2, groups, one_group, acc)
-    scale_ref[...] = jnp.broadcast_to(jnp.where(sub8[:, :1] < draft, 1.0 / jnp.sum(acc, axis=1, keepdims=True), 1.0), (SUB, LANES))
-
+    pe_ref[pl.ds(total_rows * SUB, SUB), :] = jnp.broadcast_to(jnp.where(sub8[:, :1] < draft, 1.0 / jnp.sum(acc, axis=1, keepdims=True), 1.0), (SUB, LANES))
+
+    xcopy.wait()
     prod = jnp.ones((1, 1), f32)
     expect = jnp.zeros((1, 1), f32)
     lane1 = lax.broadcasted_iota(jnp.int32, (1, LANES), 1)
@@ -266,7 +269,7 @@
         expect = expect + prod
         out_row = jnp.where(lane1 == j, ratio, out_row)
     out_row = jnp.where(lane1 == draft, expect, out_row)
-    aux_ref[...] = jnp.broadcast_to(out_row, (SUB, LANES))
+    pe_ref[pl.ds((total_rows + 1) * SUB, SUB), :] = jnp.broadcast_to(out_row, (SUB, LANES))
 
     def wait_sent(g, pos, size):
         view = send.at[pl.ds(0, others), pl.ds(pos, size), pl.ds(0, positions), :]
@@ -282,11 +285,13 @@
     pltpu.make_async_copy(stat_send.at[pl.ds(0, others)], stat_send.at[pl.ds(0, others)], tsem).wait()
 
 
-def finish_kernel(geo, pe_ref, scale_ref, aux_ref, res_ref, bonus_ref, acc_ref, exp_ref, stage, sem):
+def finish_kernel(geo, pe_ref, res_ref, bonus_ref, acc_ref, exp_ref, stage, sem):
     total_rows, padded, draft, cuts = geo
-    acc_ref[...] = aux_ref[0:1, 0:draft]
-    exp_ref[...] = aux_ref[0:1, draft:draft + 1]
-    scales = [jnp.broadcast_to(scale_ref[j:j + 1, :], (SUB, LANES)) for j in range(draft)]
+    aux = (total_rows + 1) * SUB
+    acc_ref[...] = pe_ref[aux:aux + 1, 0:draft]
+    exp_ref[...] = pe_ref[aux:aux + 1, draft:draft + 1]
+    scale = total_rows * SUB
+    scales = [jnp.broadcast_to(pe_ref[scale + j:scale + j + 1, :], (SUB, LANES)) for j in range(draft)]
     copies = []
     for c, (lo, hi) in enumerate(cuts):
         @pl.loop(lo // SUB, -(-hi // SUB))
@@ -313,7 +318,7 @@
         vocab = q_rows.shape[2]
         slots = -(-width // LANES)
         total_rows = vocab // LANES
-        padded = -(-total_rows // SUB) * SUB
+        padded = -(-(total_rows + 2) // SUB) * SUB
         slack = LANES - (width - (slots - 1) * LANES)
         h = jnp.transpose(hidden, (1, 0, 2)).reshape(positions * batch, depth)
         w = jnp.transpose(w_shard)
@@ -324,15 +329,15 @@
         hbm = pl.BlockSpec(memory_space=pltpu.HBM)
         vmem = pl.BlockSpec(memory_space=pltpu.VMEM)
         geo = (n, width, slots, slots, draft, batch, total_rows)
-        pe, aux, scale = pl.pallas_call(
+        w, h, q, x = (pltpu.with_memory_space_constraint(a, pltpu.HBM) for a in (w, h, q, x))
+        pe = pl.pallas_call(
             functools.partial(exchange_kernel, geo),
             name="verify_exchange",
-            out_shape=(jax.ShapeDtypeStruct((padded * SUB, LANES), f32),
-                       jax.ShapeDtypeStruct((SUB, LANES), f32),
-                       jax.ShapeDtypeStruct((SUB, LANES), f32)),
-            in_specs=[hbm, hbm, hbm, pl.BlockSpec(memory_space=pltpu.SMEM)],
-            out_specs=(vmem, vmem, vmem),
+            out_shape=jax.ShapeDtypeStruct((padded * SUB, LANES), f32),
+            in_specs=[hbm, hbm, hbm, hbm],
+            out_specs=vmem,
             scratch_shapes=[
+                pltpu.SMEM((draft, batch), jnp.int32),
                 pltpu.VMEM((positions * batch, depth), jnp.bfloat16),
                 pltpu.VMEM((SUB * batch, depth), jnp.bfloat16),
                 pltpu.VMEM((5 * LANES + slack, depth), jnp.bfloat16),
@@ -343,6 +348,7 @@
                 pltpu.VMEM((batch, 1, LANES), f32),
                 pltpu.VMEM((n, 1, LANES), f32),
                 pltpu.VMEM((batch, SUB, LANES), f32),
+                pltpu.SemaphoreType.DMA,
                 pltpu.SemaphoreType.DMA,
                 pltpu.SemaphoreType.DMA((3,)),
                 pltpu.SemaphoreType.DMA((NBUF,)),
@@ -363,10 +369,11 @@
                        jax.ShapeDtypeStruct((total_rows, 1, LANES), f32),
                        jax.ShapeDtypeStruct((1, draft), f32),
                        jax.ShapeDtypeStruct((1, 1), f32)),
-            in_specs=[vmem, vmem, vmem],
+            in_specs=[vmem],
             out_specs=(hbm, hbm, vmem, vmem),
             scratch_shapes=[pltpu.VMEM((positions, padded, LANES), f32), pltpu.SemaphoreType.DMA((len(cuts), positions))],
-        )(pe, scale, aux)
+            compiler_params=pltpu.CompilerParams(vmem_limit_bytes=16 * 2**20),
+        )(pe)
         residual = jnp.transpose(res.reshape(draft, 1, vocab), (1, 0, 2))
         return accept, expected.reshape(1), residual, bonus.reshape(1, vocab)
 

time: 93.9 us -> 86.4 us (0.920)
  local copies, waits for them, and re-layouts: 6.63 us -> 0 us
    unnamed x12 -> x0, local copies, waits for them, and re-layouts: 6.63 us -> none
    pallas_call x1, Pallas kernels: 5.17 us -> 3 us  [local_step(): pl.pallas_call(functools.partial(finish_kernel, (total_rows, padded, draf...]
    pallas_call x1, Pallas kernels: 81.3 us -> 82.7 us  [local_step(): pl.pallas_call(functools.partial(exchange_kernel, geo), name='verify_exch...]
where the time goes in v2:
time: 86.4 us; the launch traced here: 86.3 us
  Pallas kernels  85.7 us (99%)
    pallas_call x1, Pallas kernels, local_step(): pl.pallas_call(functools.partial(exchange_kernel, geo), name='verify_exch...  82.7 us
    pallas_call x1, Pallas kernels, local_step(): pl.pallas_call(functools.partial(finish_kernel, (total_rows, padded, draf...  3 us

profile of v2, /device:TPU:21, one launch (start us, length us, event | category | flops | bytes accessed | tf_op | source)
XLA Modules:
  0.0 86.3 jit_solution(5156397118676448779)
XLA Ops:
  0.6 82.7 %verify_exchange.1.pe_ref = f32[8064,128]{1,0:T(8,128)S(1)} custom-call(bf16[8016,4096]{1,0:T(8,128)(2,1)} %bitcast.9, bf16[96,4096]{1,0:T(8,128)(2,1)} %bitcast.11, f32[5,1002,1,128]{3,2,1,0:T(1,128)} %bitcast.10, s32[5,16]{1,0:T(8,128)} %bitcast.12), custom_call_target="tpu_custom_call" | custom-call | tf_op jit(solution)/shard_map/verify_exchange/pallas_call | solution.py:333
  83.3 3.0 %verify_finish.1 = (f32[5,1002,1,128]{3,2,1,0:T(1,128)}, f32[1002,1,128]{2,1,0:T(1,128)}, f32[1,5]{1,0:T(1,128)}, f32[1,1]{1,0:T(1,128)}) custom-call(f32[8064,128]{1,0:T(8,128)S(1)} %verify_exchange.1.pe_ref), custom_call_target="tpu_custom_call" | custom-call | tf_op jit(solution)/shard_map/verify_finish/pallas_call | solution.py:365

commit v3 on v2

v3 whole, which is shorter than its diff:
```python
import functools

import jax
import jax.numpy as jnp
from jax import lax
from jax.experimental import pallas as pl
from jax.experimental.pallas import tpu as pltpu
from jax.sharding import PartitionSpec as P

INV_TEMP = 1.25
LANES = 128
SUB = 8
TILE_ROWS = 2
NBUF = 4
GROUP_TILES = 4
AXIS = "tp"
MESH = pl.DeviceIdType.MESH


def group_plan(slots):
    main = slots - 2
    plan = [(0, 1), (1, TILE_ROWS), (1 + TILE_ROWS, TILE_ROWS), (main, 2)]
    pos, rows = 1 + 2 * TILE_ROWS, GROUP_TILES * TILE_ROWS
    while pos < main:
        plan.append((pos, rows))
        pos += rows
    assert pos == main
    last, size = plan.pop()
    return plan + [(last, size - TILE_ROWS), (last + size - TILE_ROWS, TILE_ROWS)]


def exchange_kernel(geo, w_ref, h_ref, q_ref, x_hbm, pe_ref,
                    x_ref, hbuf, fbuf, ebuf, wbuf, send, recv, qbuf, stat_send, stat_recv, peak, peak_t,
                    xsem, hsem, esem, wsem, qsem, ssem, rsem, tsem, usem):
    n, width, slots, draft, batch, total_rows, pitch, plan = geo
    f32 = jnp.float32
    me = lax.axis_index(AXIS)
    chip, core = me // 2, lax.rem(me, 2)
    chips = n // 2
    off = pl.multiple_of(lax.rem(me * width, LANES), 16)
    last_fill = width - (slots - 1) * LANES
    slack = LANES - last_fill
    tail = pl.multiple_of(jnp.maximum(off - slack, 0), 16)
    positions = draft + 1
    halves = batch // SUB
    main = slots - 2
    others = n - 1
    groups = len(plan)

    hcopy = pltpu.make_async_copy(h_ref, hbuf, hsem)
    hcopy.start()
    fcopy = pltpu.make_async_copy(w_ref.at[pl.ds(pl.multiple_of(LANES - off, 16), LANES)], fbuf, esem.at[3])
    fcopy.start()

    barrier = pltpu.get_barrier_semaphore()
    for k in range(1, n):
        pl.semaphore_signal(barrier, inc=1, device_id={AXIS: lax.rem(me + k, n)}, device_id_type=MESH)

    tile_cols = TILE_ROWS * LANES
    tiles = (main - 1) // TILE_ROWS

    def w_copy(t):
        start = pl.multiple_of(2 * LANES - off + t * tile_cols, 16)
        slot = lax.rem(t, NBUF)
        return pltpu.make_async_copy(w_ref.at[pl.ds(start, tile_cols)], wbuf.at[slot], wsem.at[slot])

    w_copy(0).start()
    e1 = pltpu.make_async_copy(w_ref.at[pl.ds(0, LANES)], ebuf.at[pl.ds(pl.multiple_of(LANES + off, 16), LANES)], esem.at[0])
    e2 = pltpu.make_async_copy(w_ref.at[pl.ds(width - LANES, LANES)], ebuf.at[pl.ds(tail, LANES)], esem.at[1])
    want = (slots - 1) * LANES - off
    src3 = pl.multiple_of(jnp.minimum(want, width - LANES), 16)
    dst3 = pl.multiple_of(3 * LANES + slack + (src3 - want), 16)
    e3 = pltpu.make_async_copy(w_ref.at[pl.ds(src3, LANES)], ebuf.at[pl.ds(dst3, LANES)], esem.at[2])
    xcopy = pltpu.make_async_copy(x_hbm, x_ref, xsem)

    order = []
    for d in range(chips // 2, 0, -1):
        order += [(d, 0), (d, 1)]
        if 2 * d != chips:
            order += [(chips - d, 0), (chips - d, 1)]
    order.append((0, 1))

    def targets():
        for dz, dc in order:
            yield lax.rem(chip + dz, chips) * 2 + lax.rem(core + dc, 2)

    def send_group(g, pos, size):
        for tgt in targets():
            pltpu.make_async_remote_copy(
                src_ref=send.at[tgt, pl.ds(pos, size), pl.ds(0, positions), :],
                dst_ref=recv.at[me, pl.ds(pos, size), pl.ds(0, positions), :],
                send_sem=ssem.at[g], recv_sem=rsem.at[g], device_id={AXIS: tgt}, device_id_type=MESH).start()

    send_flat = send.reshape(batch * slots * SUB, LANES)

    def logits_of(block):
        z = lax.dot_general(hbuf[...], block, (((1,), (1,)), ((), ())), preferred_element_type=f32)
        return z * INV_TEMP

    def put(z, pos, ok=None):
        for r in range(positions * halves):
            j, half = r // halves, r % halves
            v = z[r * SUB:(r + 1) * SUB, :]
            send_flat[pl.ds((half * SUB * slots + pos) * SUB + j, SUB, stride=slots * SUB), :] = v
            peak[r] = jnp.maximum(peak[r], v if ok is None else jnp.where(ok, v, jnp.finfo(f32).min))
        recv[me, pos] = send[me, pos]

    peak[...] = jnp.full(peak.shape, jnp.finfo(f32).min, f32)
    hcopy.wait()
    fcopy.wait()
    w_copy(1).start()
    put(logits_of(fbuf[...]), 0)
    w_copy(2).start()
    e1.start()
    e2.start()
    e3.start()
    xcopy.start()
    pl.semaphore_wait(barrier, n - 1)
    send_group(0, *plan[0])

    def tile(t):
        @pl.when(t + NBUF - 1 < tiles)
        def _():
            w_copy(t + NBUF - 1).start()

        w_copy(t).wait()
        z = logits_of(wbuf[lax.rem(t, NBUF)])
        for i in range(TILE_ROWS):
            put(z[:, i * LANES:(i + 1) * LANES], 1 + t * TILE_ROWS + i)

    @pl.loop(0, 2)
    def _(t):
        tile(t)
        send_group(1 + t, 1 + t * TILE_ROWS, TILE_ROWS)

    lane8 = lax.broadcasted_iota(jnp.int32, (SUB, LANES), 1)
    sub8 = lax.broadcasted_iota(jnp.int32, (SUB, LANES), 0)
    ok_first = jnp.logical_or(lane8 >= off, lane8 < tail)
    ok_last = lane8 < jnp.minimum(off + last_fill, LANES)
    e1.wait()
    e2.wait()
    e3.wait()
    put(logits_of(ebuf[pl.ds(LANES, LANES), :]), main, ok_first)
    put(logits_of(ebuf[pl.ds(3 * LANES + slack, LANES), :]), main + 1, ok_last)
    send_group(3, *plan[3])

    big_rows = GROUP_TILES * TILE_ROWS
    held = 3

    @pl.loop(2, tiles)
    def _(t):
        tile(t)
        done = (t - 1) // GROUP_TILES

        @pl.when(jnp.logical_and(lax.rem(t - 1, GROUP_TILES) == 0, done <= groups - held - 4))
        def _():
            send_group(3 + done, 1 + 2 * TILE_ROWS + (done - 1) * big_rows, big_rows)

    for j in range(draft):
        pltpu.make_async_copy(q_ref.at[j, :, 0, :], qbuf.at[:, j, :], qsem.at[j]).start()

    diag_m = lane8 == sub8
    diag_l = lane8 == sub8 + SUB
    for r in range(positions * halves):
        peak_t[pl.ds((r % halves) * SUB * SUB + r // halves, SUB, stride=SUB), :] = peak[r]

    @pl.loop(0, batch)
    def _(b):
        m = jnp.max(peak_t[pl.ds(pl.multiple_of(b * SUB, SUB), SUB), :], axis=1, keepdims=True)
        accs = [jnp.where(ok_first, jnp.exp(send[b, main] - m), 0.0), jnp.where(ok_last, jnp.exp(send[b, main + 1] - m), 0.0),
                jnp.exp(send[b, 0] - m), jnp.exp(send[b, 1] - m)]
        for r in range(2, main):
            accs[r % 4] = accs[r % 4] + jnp.exp(send[b, r] - m)
        l = jnp.sum((accs[0] + accs[1]) + (accs[2] + accs[3]), axis=1, keepdims=True)
        row = jnp.where(diag_m, m, 0.0) + jnp.where(diag_l, l, 0.0)
        stat_send[b] = jnp.sum(row, axis=0, keepdims=True)

    stat_recv[me] = stat_send[me]
    for tgt in targets():
        pltpu.make_async_remote_copy(src_ref=stat_send.at[tgt], dst_ref=stat_recv.at[me], send_sem=tsem, recv_sem=usem,
                                     device_id={AXIS: tgt}, device_id_type=MESH).start()
    for g in range(groups - held, groups):
        send_group(g, *plan[g])

    pltpu.make_async_copy(stat_recv.at[pl.ds(0, others)], stat_recv.at[pl.ds(0, others)], usem).wait()
    stats = [stat_recv[s] for s in range(n)]
    top = functools.reduce(jnp.maximum, stats)
    tot = jnp.zeros_like(top)
    for s in range(n):
        tot = tot + jnp.exp(stats[s] - top) * pltpu.roll(stats[s], LANES - SUB, 1)

    def spread(row):
        return jnp.sum(jnp.where(diag_m, row, 0.0), axis=1, keepdims=True)

    peak_g = jnp.broadcast_to(spread(top), (SUB, LANES))
    inv_sum = jnp.broadcast_to(1.0 / spread(tot), (SUB, LANES))

    for j in range(draft):
        pltpu.make_async_copy(q_ref.at[j, :, 0, :], qbuf.at[:, j, :], qsem.at[j]).wait()
    xcopy.wait()

    is_draft = sub8 < draft

    def excess_of(z, row):
        p = jnp.exp(z - peak_g) * inv_sum
        e = jnp.maximum(p - jnp.where(is_draft, qbuf[row], 0.0), 0.0)
        pe_ref[pl.ds(row, SUB, stride=pitch), :] = e
        return e

    def wait_group(g, pos, size):
        view = recv.at[pl.ds(0, others), pl.ds(pos, size), pl.ds(0, positions), :]
        pltpu.make_async_copy(view, view, rsem.at[g]).wait()

    def main_rows(pos, size, acc):
        def one(s, acc):
            base = (s * width) // LANES + pos + 1
            es = [excess_of(recv[s, pos + i], base + i) for i in range(size)]
            while len(es) > 1:
                es = [es[i] + es[i + 1] for i in range(0, len(es) - 1, 2)] + ([es[-1]] if len(es) % 2 else [])
            return acc + es[0]
        return lax.fori_loop(0, n, one, acc)

    acc = jnp.zeros((SUB, LANES), f32)
    for g in range(3):
        wait_group(g, *plan[g])
        acc = main_rows(*plan[g], acc)

    parts = {}
    for s in range(n):
        first, o = (s * width) // LANES, (s * width) % LANES
        t_s = max(o - slack, 0)
        parts.setdefault(first, []).append((s, main, o, LANES))
        if t_s:
            parts.setdefault(first + slots, []).append((s, main, 0, t_s))
        parts.setdefault(first + slots - 1, []).append((s, main + 1, 0, min(LANES, o + last_fill)))
    wait_group(3, *plan[3])
    for row, pieces in sorted(parts.items()):
        z = recv[pieces[0][0], pieces[0][1]]
        for s, pos, lo, hi in pieces[1:]:
            z = jnp.where(jnp.logical_and(lane8 >= lo, lane8 < hi), recv[s, pos], z)
        acc = acc + excess_of(z, row)

    def one_group(g, acc):
        pos = 1 + 2 * TILE_ROWS + (g - 4) * big_rows
        wait_group(g, pos, big_rows)
        return main_rows(pos, big_rows, acc)

    acc = lax.fori_loop(4, groups - 2, one_group, acc)
    for g in range(groups - 2, groups):
        wait_group(g, *plan[g])
        acc = main_rows(*plan[g], acc)
    spare = pitch - SUB
    pe_ref[pl.ds(spare, SUB), :] = jnp.broadcast_to(1.0 / jnp.sum(acc, axis=1, keepdims=True), (SUB, LANES))

    prod = jnp.ones((1, 1), f32)
    expect = jnp.zeros((1, 1), f32)
    lane1 = lax.broadcasted_iota(jnp.int32, (1, LANES), 1)
    out_row = jnp.zeros((1, LANES), f32)
    for j in range(draft):
        x = x_ref[j, me]
        s = x // width
        row = x // LANES
        slot = row - (s * width) // LANES
        pos = jnp.where(jnp.logical_or(slot == 0, slot == slots), main, jnp.where(slot == slots - 1, main + 1, slot - 1))
        here = jnp.logical_and(sub8 == j, lane8 == lax.rem(x, LANES))
        p = jnp.exp(recv[s, pos] - peak_g) * inv_sum

        def at_token(v):
            return jnp.sum(jnp.sum(jnp.where(here, v, 0.0), axis=1, keepdims=True), axis=0, keepdims=True)

        ratio = jnp.minimum(1.0, at_token(p) / at_token(qbuf[row]))
        prod = prod * ratio
        expect = expect + prod
        out_row = jnp.where(lane1 == j, ratio, out_row)
    out_row = jnp.where(lane1 == draft, expect, out_row)
    pe_ref[pl.ds(pitch + spare, SUB), :] = jnp.broadcast_to(out_row, (SUB, LANES))

    for g in range(groups):
        pos, size = plan[g]
        view = send.at[pl.ds(0, others), pl.ds(pos, size), pl.ds(0, positions), :]
        pltpu.make_async_copy(view, view, ssem.at[g]).wait()
    pltpu.make_async_copy(stat_send.at[pl.ds(0, others)], stat_send.at[pl.ds(0, others)], tsem).wait()


def finish_kernel(geo, pe_ref, res_ref, bonus_ref, acc_ref, exp_ref, stage, sem):
    total_rows, pitch, draft, cuts = geo
    copies = [pltpu.make_async_copy(pe_ref.at[pl.ds(draft * pitch, total_rows), :], bonus_ref.at[:, 0, :], sem.at[draft * len(cuts)])]
    copies[0].start()
    spare = pitch - SUB
    for j in range(draft):
        scale = jnp.broadcast_to(pe_ref[spare + j:spare + j + 1, :], (SUB, LANES))
        for c, (lo, hi) in enumerate(cuts):
            up = -(-hi // SUB) * SUB
            block = pe_ref[j * pitch + lo:j * pitch + up, :].reshape((up - lo) // SUB, SUB, LANES)
            stage[j, lo:up, :] = (block * scale[None]).reshape(up - lo, LANES)
            copies.append(pltpu.make_async_copy(stage.at[j, pl.ds(lo, hi - lo), :], res_ref.at[j, pl.ds(lo, hi - lo), 0, :],
                                                sem.at[j * len(cuts) + c]))
            copies[-1].start()
    aux = pitch + spare
    acc_ref[...] = pe_ref[aux:aux + 1, 0:draft]
    exp_ref[...] = pe_ref[aux:aux + 1, draft:draft + 1]
    for cp in copies:
        cp.wait()


def solution(mesh):
    n = mesh.shape[AXIS]

    def local_step(hidden, w_shard, q_rows, x_group):
        f32 = jnp.float32
        batch, positions, depth = hidden.shape
        draft = positions - 1
        width = w_shard.shape[1]
        vocab = q_rows.shape[2]
        slots = -(-width // LANES)
        total_rows = vocab // LANES
        padded = -(-total_rows // SUB) * SUB
        pitch = padded + SUB
        slack = slots * LANES - width
        plan = group_plan(slots)
        groups = len(plan)
        h = jnp.transpose(hidden, (1, 0, 2)).reshape(positions * batch, depth)
        w = jnp.transpose(w_shard)
        q = jnp.transpose(q_rows, (1, 0, 2)).reshape(draft, total_rows, 1, LANES)
        x = jnp.transpose(x_group)
        hbm = pl.BlockSpec(memory_space=pltpu.HBM)
        vmem = pl.BlockSpec(memory_space=pltpu.VMEM)
        w, h, q, x = (pltpu.with_memory_space_constraint(a, pltpu.HBM) for a in (w, h, q, x))
        geo = (n, width, slots, draft, batch, total_rows, pitch, plan)
        pe = pl.pallas_call(
            functools.partial(exchange_kernel, geo),
            name="verify_exchange",
            out_shape=jax.ShapeDtypeStruct((SUB * pitch, LANES), f32),
            in_specs=[hbm, hbm, hbm, hbm],
            out_specs=vmem,
            scratch_shapes=[
                pltpu.SMEM((draft, batch), jnp.int32),
                pltpu.VMEM((positions * batch, depth), jnp.bfloat16),
                pltpu.VMEM((LANES, depth), jnp.bfloat16),
                pltpu.VMEM((4 * LANES + slack, depth), jnp.bfloat16),
                pltpu.VMEM((NBUF, TILE_ROWS * LANES, depth), jnp.bfloat16),
                pltpu.VMEM((batch, slots, SUB, LANES), f32),
                pltpu.VMEM((n, slots, SUB, LANES), f32),
                pltpu.VMEM((total_rows, SUB, LANES), f32),
                pltpu.VMEM((batch, 1, LANES), f32),
                pltpu.VMEM((n, 1, LANES), f32),
                pltpu.VMEM((positions * batch // SUB, SUB, LANES), f32),
                pltpu.VMEM((batch * SUB, LANES), f32),
                pltpu.SemaphoreType.DMA,
                pltpu.SemaphoreType.DMA,
                pltpu.SemaphoreType.DMA((4,)),
                pltpu.SemaphoreType.DMA((NBUF,)),
                pltpu.SemaphoreType.DMA((draft,)),
                pltpu.SemaphoreType.DMA((groups,)),
                pltpu.SemaphoreType.DMA((groups,)),
                pltpu.SemaphoreType.DMA,
                pltpu.SemaphoreType.DMA,
            ],
            compiler_params=pltpu.CompilerParams(collective_id=0, has_side_effects=True, vmem_limit_bytes=40 * 2**20),
        )(w, h, q, x)
        cut = padded // 2 // SUB * SUB
        cuts = ((0, cut), (cut, total_rows))
        res, bonus, accept, expected = pl.pallas_call(
            functools.partial(finish_kernel, (total_rows, pitch, draft, cuts)),
            name="verify_finish",
            out_shape=(jax.ShapeDtypeStruct((draft, total_rows, 1, LANES), f32),
                       jax.ShapeDtypeStruct((total_rows, 1, LANES), f32),
                       jax.ShapeDtypeStruct((1, draft), f32),
                       jax.ShapeDtypeStruct((1, 1), f32)),
            in_specs=[vmem],
            out_specs=(hbm, hbm, vmem, vmem),
            scratch_shapes=[pltpu.VMEM((draft, padded, LANES), f32), pltpu.SemaphoreType.DMA((draft * len(cuts) + 1,))],
            compiler_params=pltpu.CompilerParams(vmem_limit_bytes=16 * 2**20),
        )(pe)
        residual = jnp.transpose(res.reshape(draft, 1, vocab), (1, 0, 2))
        return accept, expected.reshape(1), residual, bonus.reshape(1, vocab)

    return jax.shard_map(local_step, mesh=mesh,
                         in_specs=(P("dp", None, None), P(None, AXIS), P(("dp", AXIS), None, None), P("dp", None)),
                         out_specs=(P(("dp", AXIS), None), P(("dp", AXIS)), P(("dp", AXIS), None, None), P(("dp", AXIS), None)),
                         check_vma=False)
```

time: 86.4 us -> 83.5 us (0.966)
  Pallas kernels: 85.7 us -> 82.4 us
    pallas_call x1, Pallas kernels: 82.7 us -> 80.2 us  [local_step(): pl.pallas_call(functools.partial(exchange_kernel, geo), name='verify_exch...]
where the time goes in v3:
time: 83.5 us; the launch traced here: 83 us
  Pallas kernels  82.4 us (99%)
    pallas_call x1, Pallas kernels, local_step(): pl.pallas_call(functools.partial(exchange_kernel, geo), name='verify_exch...  80.2 us
    pallas_call x1, Pallas kernels, local_step(): pl.pallas_call(functools.partial(finish_kernel, (total_rows, pitch, draft...  2.24 us

profile of v3, /device:TPU:21, one launch (start us, length us, event | category | flops | bytes accessed | tf_op | source)
XLA Modules:
  0.0 83.0 jit_solution(6538219612772471483)
XLA Ops:
  0.6 80.2 %verify_exchange.1.pe_ref = f32[8128,128]{1,0:T(8,128)S(1)} custom-call(bf16[8016,4096]{1,0:T(8,128)(2,1)} %bitcast.9, bf16[96,4096]{1,0:T(8,128)(2,1)} %bitcast.11, f32[5,1002,1,128]{3,2,1,0:T(1,128)} %bitcast.10, s32[5,16]{1,0:T(8,128)} %bitcast.12), custom_call_target="tpu_custom_call" | custom-call | tf_op jit(solution)/shard_map/verify_exchange/pallas_call | solution.py:330
  80.8 2.2 %verify_finish.1 = (f32[5,1002,1,128]{3,2,1,0:T(1,128)}, f32[1002,1,128]{2,1,0:T(1,128)}, f32[1,5]{1,0:T(1,128)}, f32[1,1]{1,0:T(1,128)}) custom-call(f32[8128,128]{1,0:T(8,128)S(1)} %verify_exchange.1.pe_ref), custom_call_target="tpu_custom_call" | custom-call | tf_op jit(solution)/shard_map/verify_finish/pallas_call | solution.py:363

commit v4 on v3

v4 whole, which is shorter than its diff:
```python
import functools

import jax
import jax.numpy as jnp
from jax import lax
from jax.experimental import pallas as pl
from jax.experimental.pallas import tpu as pltpu
from jax.sharding import PartitionSpec as P

INV_TEMP = 1.25
LANES = 128
SUB = 8
TILE_ROWS = 2
NBUF = 4
AXIS = "tp"
MESH = pl.DeviceIdType.MESH


GROUPS = (("F",), (1,), (2,), (4,), (8,), ("E", 7), (8,))
HELD = 2


def group_plan(slots):
    pos = tile = 0
    edge = None
    plan = []
    for group in GROUPS:
        start, first, has_edge = pos, tile, False
        for item in group:
            if item == "F":
                assert pos == 0
                pos += 1
            elif item == "E":
                assert pos == start
                edge, has_edge = pos, True
                pos += 2
            else:
                tile += item
                pos += item * TILE_ROWS
        plan.append((start, pos - start, first, tile - first, has_edge))
    assert pos == slots and edge is not None
    return tuple(plan), edge


def exchange_kernel(geo, w_ref, h_ref, q_ref, x_hbm, pe_ref,
                    x_ref, hbuf, fbuf, ebuf, wbuf, send, recv, qbuf, peak, peak_t,
                    xsem, hsem, esem, wsem, qsem, ssem, rsem, lsem):
    n, width, slots, draft, batch, total_rows, pitch, plan, edge = geo
    f32 = jnp.float32
    me = lax.axis_index(AXIS)
    chip, core = me // 2, lax.rem(me, 2)
    chips = n // 2
    off = pl.multiple_of(lax.rem(me * width, LANES), 16)
    last_fill = width - (slots - 1) * LANES
    slack = LANES - last_fill
    tail = pl.multiple_of(jnp.maximum(off - slack, 0), 16)
    positions = draft + 1
    halves = batch // SUB
    main = slots - 2
    others = n - 1
    groups = len(plan)

    hcopy = pltpu.make_async_copy(h_ref, hbuf, hsem)
    hcopy.start()
    fcopy = pltpu.make_async_copy(w_ref.at[pl.ds(pl.multiple_of(LANES - off, 16), LANES)], fbuf, esem.at[3])
    fcopy.start()

    barrier = pltpu.get_barrier_semaphore()
    for k in range(1, n):
        pl.semaphore_signal(barrier, inc=1, device_id={AXIS: lax.rem(me + k, n)}, device_id_type=MESH)

    tile_cols = TILE_ROWS * LANES
    tiles = (main - 1) // TILE_ROWS

    def w_copy(t):
        start = pl.multiple_of(2 * LANES - off + t * tile_cols, 16)
        slot = lax.rem(t, NBUF)
        return pltpu.make_async_copy(w_ref.at[pl.ds(start, tile_cols)], wbuf.at[slot], wsem.at[slot])

    w_copy(0).start()
    e1 = pltpu.make_async_copy(w_ref.at[pl.ds(0, LANES)], ebuf.at[pl.ds(pl.multiple_of(LANES + off, 16), LANES)], esem.at[0])
    e2 = pltpu.make_async_copy(w_ref.at[pl.ds(width - LANES, LANES)], ebuf.at[pl.ds(tail, LANES)], esem.at[1])
    want = (slots - 1) * LANES - off
    src3 = pl.multiple_of(jnp.minimum(want, width - LANES), 16)
    dst3 = pl.multiple_of(3 * LANES + slack + (src3 - want), 16)
    e3 = pltpu.make_async_copy(w_ref.at[pl.ds(src3, LANES)], ebuf.at[pl.ds(dst3, LANES)], esem.at[2])
    xcopy = pltpu.make_async_copy(x_hbm, x_ref, xsem)

    hops = []
    for d in range(chips // 2, 0, -1):
        hops += [d] if 2 * d == chips else [d, chips - d]
    order = [(d, c) for c in (1, 0) for d in hops] + [(0, 1)]

    def targets():
        for dz, dc in order:
            yield lax.rem(chip + dz, chips) * 2 + lax.rem(core + dc, 2)

    def send_group(g):
        pos, size = plan[g][:2]
        for k, tgt in enumerate(targets()):
            pltpu.make_async_remote_copy(
                src_ref=send.at[tgt, pl.ds(pos, size), pl.ds(0, positions), :],
                dst_ref=recv.at[me, pl.ds(pos, size), pl.ds(0, positions), :],
                send_sem=ssem.at[g], recv_sem=lsem.at[k] if g == groups - 1 else rsem.at[g], device_id={AXIS: tgt}, device_id_type=MESH).start()

    send_flat = send.reshape(batch * slots * SUB, LANES)

    def logits_of(block):
        z = lax.dot_general(hbuf[...], block, (((1,), (1,)), ((), ())), preferred_element_type=f32)
        return z * INV_TEMP

    def put(z, pos, ok=None):
        for r in range(positions * halves):
            j, half = r // halves, r % halves
            v = z[r * SUB:(r + 1) * SUB, :]
            send_flat[pl.ds((half * SUB * slots + pos) * SUB + j, SUB, stride=slots * SUB), :] = v
            peak[r] = jnp.maximum(peak[r], v if ok is None else jnp.where(ok, v, jnp.finfo(f32).min))
        recv[me, pos] = send[me, pos]

    peak[...] = jnp.full(peak.shape, jnp.finfo(f32).min, f32)
    hcopy.wait()
    fcopy.wait()
    w_copy(1).start()
    put(logits_of(fbuf[...]), 0)
    w_copy(2).start()
    e1.start()
    e2.start()
    e3.start()
    xcopy.start()

    lane8 = lax.broadcasted_iota(jnp.int32, (SUB, LANES), 1)
    sub8 = lax.broadcasted_iota(jnp.int32, (SUB, LANES), 0)
    ok_first = jnp.logical_or(lane8 >= off, lane8 < tail)
    ok_last = lane8 < jnp.minimum(off + last_fill, LANES)

    def make_group(g):
        start, _, first, count, has_edge = plan[g]
        if has_edge:
            e1.wait()
            e2.wait()
            e3.wait()
            put(logits_of(ebuf[pl.ds(LANES, LANES), :]), edge, ok_first)
            put(logits_of(ebuf[pl.ds(3 * LANES + slack, LANES), :]), edge + 1, ok_last)
        base = start + (2 if has_edge else 0) + (1 if g == 0 else 0) - first * TILE_ROWS
        if not count:
            return

        @pl.loop(first, first + count)
        def _(t):
            @pl.when(t + NBUF - 1 < tiles)
            def _():
                w_copy(t + NBUF - 1).start()

            w_copy(t).wait()
            z = logits_of(wbuf[lax.rem(t, NBUF)])
            for i in range(TILE_ROWS):
                put(z[:, i * LANES:(i + 1) * LANES], base + t * TILE_ROWS + i)

    for g in range(groups):
        make_group(g)
        if g == 0:
            pl.semaphore_wait(barrier, n - 1)
        if g < groups - HELD:
            send_group(g)

    for j in range(draft):
        pltpu.make_async_copy(q_ref.at[j, :, 0, :], qbuf.at[:, j, :], qsem.at[j]).start()

    gap_first = jnp.where(off >= slack, off - 2, LANES)
    gap_last = jnp.where(off >= slack, LANES, LANES - 2)
    for r in range(positions * halves):
        peak_t[pl.ds((r % halves) * SUB * SUB + r // halves, SUB, stride=SUB), :] = peak[r]

    @pl.loop(0, batch)
    def _(b):
        m = jnp.max(peak_t[pl.ds(pl.multiple_of(b * SUB, SUB), SUB), :], axis=1, keepdims=True)
        accs = [jnp.where(ok_first, jnp.exp(send[b, edge] - m), 0.0), jnp.where(ok_last, jnp.exp(send[b, edge + 1] - m), 0.0)] + [0.0] * 2
        for r in [r for r in range(slots) if not edge <= r < edge + 2]:
            accs[r % 4] = accs[r % 4] + jnp.exp(send[b, r] - m)
        l = jnp.sum((accs[0] + accs[1]) + (accs[2] + accs[3]), axis=1, keepdims=True)
        for at, gap in ((edge, gap_first), (edge + 1, gap_last)):
            send[b, at] = jnp.where(lane8 == gap, m, jnp.where(lane8 == gap + 1, l, send[b, at]))

    for at in (edge, edge + 1):
        recv[me, at] = send[me, at]
    for g in range(groups - HELD, groups):
        send_group(g)

    def wait_group(g):
        pos, size = plan[g][:2]
        view = recv.at[pl.ds(0, others), pl.ds(pos, size), pl.ds(0, positions), :]
        pltpu.make_async_copy(view, view, rsem.at[g]).wait()

    edge_group = next(g for g in range(groups) if plan[g][4])
    assert groups - HELD <= edge_group < groups - 1
    wait_group(edge_group)
    stats = []
    for s in range(n):
        o = (s * width) % LANES
        at, gap = (edge, o - 2) if o >= slack else (edge + 1, LANES - 2)
        v = recv[s, at]
        stats.append((v[:, gap:gap + 1], v[:, gap + 1:gap + 2]))
    top = functools.reduce(jnp.maximum, [m for m, _ in stats])
    tot = functools.reduce(jnp.add, [l * jnp.exp(m - top) for m, l in stats])
    peak_g = jnp.broadcast_to(top, (SUB, LANES))
    inv_sum = jnp.broadcast_to(1.0 / tot, (SUB, LANES))

    for j in range(draft):
        pltpu.make_async_copy(q_ref.at[j, :, 0, :], qbuf.at[:, j, :], qsem.at[j]).wait()
    xcopy.wait()

    is_draft = sub8 < draft

    def excess_of(z, row):
        p = jnp.exp(z - peak_g) * inv_sum
        e = jnp.maximum(p - jnp.where(is_draft, qbuf[row], 0.0), 0.0)
        pe_ref[pl.ds(row, SUB, stride=pitch), :] = e
        return e

    parts = {}
    for s in range(n):
        first, o = (s * width) // LANES, (s * width) % LANES
        t_s = max(o - slack, 0)
        parts.setdefault(first, []).append((s, edge, o, LANES))
        if t_s:
            parts.setdefault(first + slots, []).append((s, edge, 0, t_s))
        parts.setdefault(first + slots - 1, []).append((s, edge + 1, 0, min(LANES, o + last_fill)))

    here, where, q_at = [], [], jnp.ones((SUB, LANES), f32)
    for j in range(draft):
        x = x_ref[j, me]
        s = x // width
        row = x // LANES
        slot = row - (s * width) // LANES
        at = jnp.where(slot <= edge, slot - 1, slot + 1)
        at = jnp.where(jnp.logical_or(slot == 0, slot == slots), edge, jnp.where(slot == slots - 1, edge + 1, at))
        where.append((s, at))
        here.append(jnp.logical_and(sub8 == j, lane8 == lax.rem(x, LANES)))
        q_at = jnp.where(here[j], qbuf[row], q_at)
    spare = pitch - SUB
    chosen = functools.reduce(jnp.logical_or, here)
    for i, v in enumerate((q_at, jnp.where(chosen, 1.0, 0.0), peak_g, inv_sum)):
        pe_ref[pl.ds((2 + i) * pitch + spare, SUB), :] = v

    def rows_of(s, pos, size, acc):
        base = (s * width) // LANES + pos + (1 if pos < edge else -1)
        es = [excess_of(recv[s, pos + i], base + i) for i in range(size)]
        while len(es) > 1:
            es = [es[i] + es[i + 1] for i in range(0, len(es) - 1, 2)] + ([es[-1]] if len(es) % 2 else [])
        return acc + es[0]

    acc = jnp.zeros((SUB, LANES), f32)
    for g in range(groups - 1):
        pos, size, _, _, has_edge = plan[g]
        if has_edge:
            for row, pieces in sorted(parts.items()):
                z = recv[pieces[0][0], pieces[0][1]]
                for s, at, lo, hi in pieces[1:]:
                    z = jnp.where(jnp.logical_and(lane8 >= lo, lane8 < hi), recv[s, at], z)
                acc = acc + excess_of(z, row)
            pos, size = pos + 2, size - 2
        else:
            wait_group(g)
        if size:
            acc = lax.fori_loop(0, n, functools.partial(lambda s, acc, pos, size: rows_of(s, pos, size, acc), pos=pos, size=size), acc)

    pos, size = plan[groups - 1][:2]
    acc = rows_of(me, pos, size, acc)
    for k, (dz, dc) in enumerate(order):
        s = lax.rem(chip - dz + chips, chips) * 2 + lax.rem(core + dc, 2)
        view = recv.at[s, pl.ds(pos, size), pl.ds(0, positions), :]
        pltpu.make_async_copy(view, view, lsem.at[k]).wait()
        acc = rows_of(s, pos, size, acc)
    pe_ref[pl.ds(spare, SUB), :] = jnp.broadcast_to(1.0 / jnp.sum(acc, axis=1, keepdims=True), (SUB, LANES))
    z_at = jnp.zeros((SUB, LANES), f32)
    for j in range(draft):
        z_at = jnp.where(here[j], recv[where[j][0], where[j][1]], z_at)
    pe_ref[pl.ds(pitch + spare, SUB), :] = z_at

    for g in range(groups):
        pos, size = plan[g][:2]
        view = send.at[pl.ds(0, others), pl.ds(pos, size), pl.ds(0, positions), :]
        pltpu.make_async_copy(view, view, ssem.at[g]).wait()


def finish_kernel(geo, pe_ref, res_ref, bonus_ref, acc_ref, exp_ref, stage, sem):
    total_rows, pitch, draft, cuts = geo
    copies = [pltpu.make_async_copy(pe_ref.at[pl.ds(draft * pitch, total_rows), :], bonus_ref.at[:, 0, :], sem.at[draft * len(cuts)])]
    copies[0].start()
    spare = pitch - SUB
    for j in range(draft):
        scale = jnp.broadcast_to(pe_ref[spare + j:spare + j + 1, :], (SUB, LANES))
        for c, (lo, hi) in enumerate(cuts):
            up = -(-hi // SUB) * SUB
            block = pe_ref[j * pitch + lo:j * pitch + up, :].reshape((up - lo) // SUB, SUB, LANES)
            stage[j, lo:up, :] = (block * scale[None]).reshape(up - lo, LANES)
            copies.append(pltpu.make_async_copy(stage.at[j, pl.ds(lo, hi - lo), :], res_ref.at[j, pl.ds(lo, hi - lo), 0, :],
                                                sem.at[j * len(cuts) + c]))
            copies[-1].start()
    z_at, q_at, chosen, peak_g, inv_sum = (pe_ref[(1 + i) * pitch + spare:(2 + i) * pitch, :] for i in range(5))
    ratio = jnp.minimum(1.0, jnp.exp(z_at - peak_g) * inv_sum / q_at)
    accept = jnp.sum(jnp.where(chosen > 0.5, ratio, 0.0), axis=1, keepdims=True)
    lane8 = lax.broadcasted_iota(jnp.int32, (SUB, LANES), 1)
    sub8 = lax.broadcasted_iota(jnp.int32, (SUB, LANES), 0)
    acc_ref[...] = jnp.sum(jnp.where(lane8 == sub8, accept, 0.0), axis=0, keepdims=True)[:, :draft]
    prod = accept[0:1, :]
    expect = prod
    for j in range(1, draft):
        prod = prod * accept[j:j + 1, :]
        expect = expect + prod
    exp_ref[...] = expect
    for cp in copies:
        cp.wait()


def solution(mesh):
    n = mesh.shape[AXIS]

    def local_step(hidden, w_shard, q_rows, x_group):
        f32 = jnp.float32
        batch, positions, depth = hidden.shape
        draft = positions - 1
        width = w_shard.shape[1]
        vocab = q_rows.shape[2]
        slots = -(-width // LANES)
        total_rows = vocab // LANES
        padded = -(-total_rows // SUB) * SUB
        pitch = padded + SUB
        slack = slots * LANES - width
        plan, edge = group_plan(slots)
        groups = len(plan)
        h = jnp.transpose(hidden, (1, 0, 2)).reshape(positions * batch, depth)
        w = jnp.transpose(w_shard)
        q = jnp.transpose(q_rows, (1, 0, 2)).reshape(draft, total_rows, 1, LANES)
        x = jnp.transpose(x_group)
        hbm = pl.BlockSpec(memory_space=pltpu.HBM)
        vmem = pl.BlockSpec(memory_space=pltpu.VMEM)
        w, h, q, x = (pltpu.with_memory_space_constraint(a, pltpu.HBM) for a in (w, h, q, x))
        geo = (n, width, slots, draft, batch, total_rows, pitch, plan, edge)
        pe = pl.pallas_call(
            functools.partial(exchange_kernel, geo),
            name="verify_exchange",
            out_shape=jax.ShapeDtypeStruct((SUB * pitch, LANES), f32),
            in_specs=[hbm, hbm, hbm, hbm],
            out_specs=vmem,
            scratch_shapes=[
                pltpu.SMEM((draft, batch), jnp.int32),
                pltpu.VMEM((positions * batch, depth), jnp.bfloat16),
                pltpu.VMEM((LANES, depth), jnp.bfloat16),
                pltpu.VMEM((4 * LANES + slack, depth), jnp.bfloat16),
                pltpu.VMEM((NBUF, TILE_ROWS * LANES, depth), jnp.bfloat16),
                pltpu.VMEM((batch, slots, SUB, LANES), f32),
                pltpu.VMEM((n, slots, SUB, LANES), f32),
                pltpu.VMEM((total_rows, SUB, LANES), f32),
                pltpu.VMEM((positions * batch // SUB, SUB, LANES), f32),
                pltpu.VMEM((batch * SUB, LANES), f32),
                pltpu.SemaphoreType.DMA,
                pltpu.SemaphoreType.DMA,
                pltpu.SemaphoreType.DMA((4,)),
                pltpu.SemaphoreType.DMA((NBUF,)),
                pltpu.SemaphoreType.DMA((draft,)),
                pltpu.SemaphoreType.DMA((groups,)),
                pltpu.SemaphoreType.DMA((groups,)),
                pltpu.SemaphoreType.DMA((n - 1,)),
            ],
            compiler_params=pltpu.CompilerParams(collective_id=0, has_side_effects=True, vmem_limit_bytes=40 * 2**20),
        )(w, h, q, x)
        cuts = ((0, total_rows),)
        res, bonus, accept, expected = pl.pallas_call(
            functools.partial(finish_kernel, (total_rows, pitch, draft, cuts)),
            name="verify_finish",
            out_shape=(jax.ShapeDtypeStruct((draft, total_rows, 1, LANES), f32),
                       jax.ShapeDtypeStruct((total_rows, 1, LANES), f32),
                       jax.ShapeDtypeStruct((1, draft), f32),
                       jax.ShapeDtypeStruct((1, 1), f32)),
            in_specs=[vmem],
            out_specs=(hbm, hbm, vmem, vmem),
            scratch_shapes=[pltpu.VMEM((draft, padded, LANES), f32), pltpu.SemaphoreType.DMA((draft * len(cuts) + 1,))],
            compiler_params=pltpu.CompilerParams(vmem_limit_bytes=16 * 2**20),
        )(pe)
        residual = jnp.transpose(res.reshape(draft, 1, vocab), (1, 0, 2))
        return accept, expected.reshape(1), residual, bonus.reshape(1, vocab)

    return jax.shard_map(local_step, mesh=mesh,
                         in_specs=(P("dp", None, None), P(None, AXIS), P(("dp", AXIS), None, None), P("dp", None)),
                         out_specs=(P(("dp", AXIS), None), P(("dp", AXIS)), P(("dp", AXIS), None, None), P(("dp", AXIS), None)),
                         check_vma=False)
```

time: 83.5 us -> 81.2 us (0.972)
  Pallas kernels: 82.4 us -> 80.5 us
    pallas_call x1, Pallas kernels: 80.2 us -> 78.3 us  [local_step(): pl.pallas_call(functools.partial(exchange_kernel, geo), name='verify_exch...]
where the time goes in v4:
time: 81.2 us; the launch traced here: 81.1 us
  Pallas kernels  80.5 us (99%)
    pallas_call x1, Pallas kernels, local_step(): pl.pallas_call(functools.partial(exchange_kernel, geo), name='verify_exch...  78.3 us
    pallas_call x1, Pallas kernels, local_step(): pl.pallas_call(functools.partial(finish_kernel, (total_rows, pitch, draft...  2.2 us

profile of v4, /device:TPU:21, one launch (start us, length us, event | category | flops | bytes accessed | tf_op | source)
XLA Modules:
  0.0 81.1 jit_solution(12142768034548790698)
XLA Ops:
  0.6 78.3 %verify_exchange.1.pe_ref = f32[8128,128]{1,0:T(8,128)S(1)} custom-call(bf16[8016,4096]{1,0:T(8,128)(2,1)} %bitcast.9, bf16[96,4096]{1,0:T(8,128)(2,1)} %bitcast.11, f32[5,1002,1,128]{3,2,1,0:T(1,128)} %bitcast.10, s32[5,16]{1,0:T(8,128)} %bitcast.12), custom_call_target="tpu_custom_call" | custom-call | tf_op jit(solution)/shard_map/verify_exchange/pallas_call | solution.py:340
  78.9 2.2 %verify_finish.1 = (f32[5,1002,1,128]{3,2,1,0:T(1,128)}, f32[1002,1,128]{2,1,0:T(1,128)}, f32[1,5]{1,0:T(1,128)}, f32[1,1]{1,0:T(1,128)}) custom-call(f32[8128,128]{1,0:T(8,128)S(1)} %verify_exchange.1.pe_ref), custom_call_target="tpu_custom_call" | custom-call | tf_op jit(solution)/shard_map/verify_finish/pallas_call | solution.py:369

commit v5 on v4

--- a/solution.py
+++ b/solution.py
@@ -16,8 +16,9 @@
 MESH = pl.DeviceIdType.MESH
 
 
-GROUPS = (("F",), (1,), (2,), (4,), (8,), ("E", 7), (8,))
+GROUPS = (("F",), (1,), (1,), (2,), (4,), (8,), ("E", 7), (7,))
 HELD = 2
+LAST_SHARE = 4
 
 
 def group_plan(slots):
@@ -62,7 +63,7 @@
 
     hcopy = pltpu.make_async_copy(h_ref, hbuf, hsem)
     hcopy.start()
-    fcopy = pltpu.make_async_copy(w_ref.at[pl.ds(pl.multiple_of(LANES - off, 16), LANES)], fbuf, esem.at[3])
+    fcopy = pltpu.make_async_copy(w_ref.at[pl.ds(pl.multiple_of(LANES - off, 16), LANES)], fbuf, hsem)
     fcopy.start()
 
     barrier = pltpu.get_barrier_semaphore()
@@ -78,12 +79,12 @@
         return pltpu.make_async_copy(w_ref.at[pl.ds(start, tile_cols)], wbuf.at[slot], wsem.at[slot])
 
     w_copy(0).start()
-    e1 = pltpu.make_async_copy(w_ref.at[pl.ds(0, LANES)], ebuf.at[pl.ds(pl.multiple_of(LANES + off, 16), LANES)], esem.at[0])
-    e2 = pltpu.make_async_copy(w_ref.at[pl.ds(width - LANES, LANES)], ebuf.at[pl.ds(tail, LANES)], esem.at[1])
+    e1 = pltpu.make_async_copy(w_ref.at[pl.ds(0, LANES)], ebuf.at[pl.ds(pl.multiple_of(LANES + off, 16), LANES)], esem)
+    e2 = pltpu.make_async_copy(w_ref.at[pl.ds(width - LANES, LANES)], ebuf.at[pl.ds(tail, LANES)], esem)
     want = (slots - 1) * LANES - off
     src3 = pl.multiple_of(jnp.minimum(want, width - LANES), 16)
     dst3 = pl.multiple_of(3 * LANES + slack + (src3 - want), 16)
-    e3 = pltpu.make_async_copy(w_ref.at[pl.ds(src3, LANES)], ebuf.at[pl.ds(dst3, LANES)], esem.at[2])
+    e3 = pltpu.make_async_copy(w_ref.at[pl.ds(src3, LANES)], ebuf.at[pl.ds(dst3, LANES)], esem)
     xcopy = pltpu.make_async_copy(x_hbm, x_ref, xsem)
 
     hops = []
@@ -101,7 +102,7 @@
             pltpu.make_async_remote_copy(
                 src_ref=send.at[tgt, pl.ds(pos, size), pl.ds(0, positions), :],
                 dst_ref=recv.at[me, pl.ds(pos, size), pl.ds(0, positions), :],
-                send_sem=ssem.at[g], recv_sem=lsem.at[k] if g == groups - 1 else rsem.at[g], device_id={AXIS: tgt}, device_id_type=MESH).start()
+                send_sem=ssem, recv_sem=lsem.at[k // LAST_SHARE] if g == groups - 1 else rsem, device_id={AXIS: tgt}, device_id_type=MESH).start()
 
     send_flat = send.reshape(batch * slots * SUB, LANES)
 
@@ -118,8 +119,8 @@
         recv[me, pos] = send[me, pos]
 
     peak[...] = jnp.full(peak.shape, jnp.finfo(f32).min, f32)
-    hcopy.wait()
-    fcopy.wait()
+    both = ebuf.at[pl.ds(0, hbuf.shape[0] + LANES)]
+    pltpu.make_async_copy(both, both, hsem).wait()
     w_copy(1).start()
     put(logits_of(fbuf[...]), 0)
     w_copy(2).start()
@@ -136,9 +137,8 @@
     def make_group(g):
         start, _, first, count, has_edge = plan[g]
         if has_edge:
-            e1.wait()
-            e2.wait()
-            e3.wait()
+            three = ebuf.at[pl.ds(0, 3 * LANES)]
+            pltpu.make_async_copy(three, three, esem).wait()
             put(logits_of(ebuf[pl.ds(LANES, LANES), :]), edge, ok_first)
             put(logits_of(ebuf[pl.ds(3 * LANES + slack, LANES), :]), edge + 1, ok_last)
         base = start + (2 if has_edge else 0) + (1 if g == 0 else 0) - first * TILE_ROWS
@@ -164,7 +164,7 @@
             send_group(g)
 
     for j in range(draft):
-        pltpu.make_async_copy(q_ref.at[j, :, 0, :], qbuf.at[:, j, :], qsem.at[j]).start()
+        pltpu.make_async_copy(q_ref.at[j, :, 0, :], qbuf.at[:, j, :], qsem).start()
 
     gap_first = jnp.where(off >= slack, off - 2, LANES)
     gap_last = jnp.where(off >= slack, LANES, LANES - 2)
@@ -186,14 +186,12 @@
     for g in range(groups - HELD, groups):
         send_group(g)
 
-    def wait_group(g):
-        pos, size = plan[g][:2]
-        view = recv.at[pl.ds(0, others), pl.ds(pos, size), pl.ds(0, positions), :]
-        pltpu.make_async_copy(view, view, rsem.at[g]).wait()
-
     edge_group = next(g for g in range(groups) if plan[g][4])
-    assert groups - HELD <= edge_group < groups - 1
-    wait_group(edge_group)
+    assert groups - HELD <= edge_group == groups - 2
+    pos, size = plan[groups - 1][:2]
+    assert pos + size == slots
+    early = recv.at[pl.ds(0, others), pl.ds(0, pos), pl.ds(0, positions), :]
+    pltpu.make_async_copy(early, early, rsem).wait()
     stats = []
     for s in range(n):
         o = (s * width) % LANES
@@ -205,8 +203,8 @@
     peak_g = jnp.broadcast_to(top, (SUB, LANES))
     inv_sum = jnp.broadcast_to(1.0 / tot, (SUB, LANES))
 
-    for j in range(draft):
-        pltpu.make_async_copy(q_ref.at[j, :, 0, :], qbuf.at[:, j, :], qsem.at[j]).wait()
+    every = qbuf.at[:, pl.ds(0, draft), :]
+    pltpu.make_async_copy(every, every, qsem).wait()
     xcopy.wait()
 
     is_draft = sub8 < draft
@@ -259,43 +257,38 @@
                     z = jnp.where(jnp.logical_and(lane8 >= lo, lane8 < hi), recv[s, at], z)
                 acc = acc + excess_of(z, row)
             pos, size = pos + 2, size - 2
-        else:
-            wait_group(g)
         if size:
             acc = lax.fori_loop(0, n, functools.partial(lambda s, acc, pos, size: rows_of(s, pos, size, acc), pos=pos, size=size), acc)
 
     pos, size = plan[groups - 1][:2]
     acc = rows_of(me, pos, size, acc)
     for k, (dz, dc) in enumerate(order):
-        s = lax.rem(chip - dz + chips, chips) * 2 + lax.rem(core + dc, 2)
-        view = recv.at[s, pl.ds(pos, size), pl.ds(0, positions), :]
-        pltpu.make_async_copy(view, view, lsem.at[k]).wait()
-        acc = rows_of(s, pos, size, acc)
+        if k % LAST_SHARE == 0:
+            view = recv.at[pl.ds(0, min(LAST_SHARE, others - k)), pl.ds(pos, size), pl.ds(0, positions), :]
+            pltpu.make_async_copy(view, view, lsem.at[k // LAST_SHARE]).wait()
+        acc = rows_of(lax.rem(chip - dz + chips, chips) * 2 + lax.rem(core + dc, 2), pos, size, acc)
     pe_ref[pl.ds(spare, SUB), :] = jnp.broadcast_to(1.0 / jnp.sum(acc, axis=1, keepdims=True), (SUB, LANES))
     z_at = jnp.zeros((SUB, LANES), f32)
     for j in range(draft):
         z_at = jnp.where(here[j], recv[where[j][0], where[j][1]], z_at)
     pe_ref[pl.ds(pitch + spare, SUB), :] = z_at
 
-    for g in range(groups):
-        pos, size = plan[g][:2]
-        view = send.at[pl.ds(0, others), pl.ds(pos, size), pl.ds(0, positions), :]
-        pltpu.make_async_copy(view, view, ssem.at[g]).wait()
+    sent = send.at[pl.ds(0, others), :, pl.ds(0, positions), :]
+    pltpu.make_async_copy(sent, sent, ssem).wait()
 
 
 def finish_kernel(geo, pe_ref, res_ref, bonus_ref, acc_ref, exp_ref, stage, sem):
     total_rows, pitch, draft, cuts = geo
-    copies = [pltpu.make_async_copy(pe_ref.at[pl.ds(draft * pitch, total_rows), :], bonus_ref.at[:, 0, :], sem.at[draft * len(cuts)])]
+    copies = [pltpu.make_async_copy(pe_ref.at[pl.ds(draft * pitch, total_rows), :], bonus_ref.at[:, 0, :], sem)]
     copies[0].start()
     spare = pitch - SUB
     for j in range(draft):
         scale = jnp.broadcast_to(pe_ref[spare + j:spare + j + 1, :], (SUB, LANES))
-        for c, (lo, hi) in enumerate(cuts):
+        for lo, hi in cuts:
             up = -(-hi // SUB) * SUB
             block = pe_ref[j * pitch + lo:j * pitch + up, :].reshape((up - lo) // SUB, SUB, LANES)
             stage[j, lo:up, :] = (block * scale[None]).reshape(up - lo, LANES)
-            copies.append(pltpu.make_async_copy(stage.at[j, pl.ds(lo, hi - lo), :], res_ref.at[j, pl.ds(lo, hi - lo), 0, :],
-                                                sem.at[j * len(cuts) + c]))
+            copies.append(pltpu.make_async_copy(stage.at[j, pl.ds(lo, hi - lo), :], res_ref.at[j, pl.ds(lo, hi - lo), 0, :], sem))
             copies[-1].start()
     z_at, q_at, chosen, peak_g, inv_sum = (pe_ref[(1 + i) * pitch + spare:(2 + i) * pitch, :] for i in range(5))
     ratio = jnp.minimum(1.0, jnp.exp(z_at - peak_g) * inv_sum / q_at)
@@ -309,8 +302,8 @@
         prod = prod * accept[j:j + 1, :]
         expect = expect + prod
     exp_ref[...] = expect
-    for cp in copies:
-        cp.wait()
+    whole = pe_ref.at[pl.ds(0, (draft + 1) * total_rows), :]
+    pltpu.make_async_copy(whole, whole, sem).wait()
 
 
 def solution(mesh):
@@ -328,7 +321,6 @@
         pitch = padded + SUB
         slack = slots * LANES - width
         plan, edge = group_plan(slots)
-        groups = len(plan)
         h = jnp.transpose(hidden, (1, 0, 2)).reshape(positions * batch, depth)
         w = jnp.transpose(w_shard)
         q = jnp.transpose(q_rows, (1, 0, 2)).reshape(draft, total_rows, 1, LANES)
@@ -356,12 +348,12 @@
                 pltpu.VMEM((batch * SUB, LANES), f32),
                 pltpu.SemaphoreType.DMA,
                 pltpu.SemaphoreType.DMA,
-                pltpu.SemaphoreType.DMA((4,)),
+                pltpu.SemaphoreType.DMA,
                 pltpu.SemaphoreType.DMA((NBUF,)),
-                pltpu.SemaphoreType.DMA((draft,)),
-                pltpu.SemaphoreType.DMA((groups,)),
-                pltpu.SemaphoreType.DMA((groups,)),
-                pltpu.SemaphoreType.DMA((n - 1,)),
+                pltpu.SemaphoreType.DMA,
+                pltpu.SemaphoreType.DMA,
+                pltpu.SemaphoreType.DMA,
+                pltpu.SemaphoreType.DMA((-(-(n - 1) // LAST_SHARE),)),
             ],
             compiler_params=pltpu.CompilerParams(collective_id=0, has_side_effects=True, vmem_limit_bytes=40 * 2**20),
         )(w, h, q, x)
@@ -375,7 +367,7 @@
                        jax.ShapeDtypeStruct((1, 1), f32)),
             in_specs=[vmem],
             out_specs=(hbm, hbm, vmem, vmem),
-            scratch_shapes=[pltpu.VMEM((draft, padded, LANES), f32), pltpu.SemaphoreType.DMA((draft * len(cuts) + 1,))],
+            scratch_shapes=[pltpu.VMEM((draft, padded, LANES), f32), pltpu.SemaphoreType.DMA],
             compiler_params=pltpu.CompilerParams(vmem_limit_bytes=16 * 2**20),
         )(pe)
         residual = jnp.transpose(res.reshape(draft, 1, vocab), (1, 0, 2))

time: 81.2 us -> 80.8 us (level)
  no operation moved by 1% of the time
where the time goes in v5:
time: 80.8 us; the launch traced here: 80.7 us
  Pallas kernels  80 us (99%)
    pallas_call x1, Pallas kernels, local_step(): pl.pallas_call(functools.partial(exchange_kernel, geo), name='verify_exch...  77.9 us
    pallas_call x1, Pallas kernels, local_step(): pl.pallas_call(functools.partial(finish_kernel, (total_rows, pitch, draft...  2.15 us

profile of v5, /device:TPU:21, one launch (start us, length us, event | category | flops | bytes accessed | tf_op | source)
XLA Modules:
  0.0 80.7 jit_solution(7663208017687230317)
XLA Ops:
  0.6 77.9 %verify_exchange.1.pe_ref = f32[8128,128]{1,0:T(8,128)S(1)} custom-call(bf16[8016,4096]{1,0:T(8,128)(2,1)} %bitcast.9, bf16[96,4096]{1,0:T(8,128)(2,1)} %bitcast.11, f32[5,1002,1,128]{3,2,1,0:T(1,128)} %bitcast.10, s32[5,16]{1,0:T(8,128)} %bitcast.12), custom_call_target="tpu_custom_call" | custom-call | tf_op jit(solution)/shard_map/verify_exchange/pallas_call | solution.py:332
  78.5 2.2 %verify_finish.1 = (f32[5,1002,1,128]{3,2,1,0:T(1,128)}, f32[1002,1,128]{2,1,0:T(1,128)}, f32[1,5]{1,0:T(1,128)}, f32[1,1]{1,0:T(1,128)}) custom-call(f32[8128,128]{1,0:T(8,128)S(1)} %verify_exchange.1.pe_ref), custom_call_target="tpu_custom_call" | custom-call | tf_op jit(solution)/shard_map/verify_finish/pallas_call | solution.py:361

commit v6 on v5

--- a/solution.py
+++ b/solution.py
@@ -16,7 +16,7 @@
 MESH = pl.DeviceIdType.MESH
 
 
-GROUPS = (("F",), (1,), (1,), (2,), (4,), (8,), ("E", 7), (7,))
+GROUPS = (("F",), (1,), (1,), (2,), (4,), (8,), ("E", 8), (6,))
 HELD = 2
 LAST_SHARE = 4
 
@@ -277,7 +277,7 @@
     pltpu.make_async_copy(sent, sent, ssem).wait()
 
 
-def finish_kernel(geo, pe_ref, res_ref, bonus_ref, acc_ref, exp_ref, stage, sem):
+def finish_kernel(geo, pe_ref, res_ref, bonus_ref, acc_hbm, exp_hbm, stage, acc_ref, exp_ref, sem, small):
     total_rows, pitch, draft, cuts = geo
     copies = [pltpu.make_async_copy(pe_ref.at[pl.ds(draft * pitch, total_rows), :], bonus_ref.at[:, 0, :], sem)]
     copies[0].start()
@@ -302,8 +302,14 @@
         prod = prod * accept[j:j + 1, :]
         expect = expect + prod
     exp_ref[...] = expect
+    acc_copy = pltpu.make_async_copy(acc_ref, acc_hbm, small.at[0])
+    exp_copy = pltpu.make_async_copy(exp_ref, exp_hbm, small.at[1])
+    acc_copy.start()
+    exp_copy.start()
     whole = pe_ref.at[pl.ds(0, (draft + 1) * total_rows), :]
     pltpu.make_async_copy(whole, whole, sem).wait()
+    acc_copy.wait()
+    exp_copy.wait()
 
 
 def solution(mesh):
@@ -366,8 +372,9 @@
                        jax.ShapeDtypeStruct((1, draft), f32),
                        jax.ShapeDtypeStruct((1, 1), f32)),
             in_specs=[vmem],
-            out_specs=(hbm, hbm, vmem, vmem),
-            scratch_shapes=[pltpu.VMEM((draft, padded, LANES), f32), pltpu.SemaphoreType.DMA],
+            out_specs=(hbm, hbm, hbm, hbm),
+            scratch_shapes=[pltpu.VMEM((draft, padded, LANES), f32), pltpu.VMEM((1, draft), f32), pltpu.VMEM((1, 1), f32),
+                            pltpu.SemaphoreType.DMA, pltpu.SemaphoreType.DMA((2,))],
             compiler_params=pltpu.CompilerParams(vmem_limit_bytes=16 * 2**20),
         )(pe)
         residual = jnp.transpose(res.reshape(draft, 1, vocab), (1, 0, 2))

time: 80.8 us -> 80 us (0.990)
  no operation moved by 1% of the time
where the time goes in v6:
time: 80 us; the launch traced here: 79.9 us
  Pallas kernels  79.3 us (99%)
    pallas_call x1, Pallas kernels, local_step(): pl.pallas_call(functools.partial(exchange_kernel, geo), name='verify_exch...  77.6 us
    pallas_call x1, Pallas kernels, local_step(): pl.pallas_call(functools.partial(finish_kernel, (total_rows, pitch, draft...  1.67 us

profile of v6, /device:TPU:21, one launch (start us, length us, event | category | flops | bytes accessed | tf_op | source)
XLA Modules:
  0.0 79.9 jit_solution(17730082932159514438)
XLA Ops:
  0.6 77.6 %verify_exchange.1.pe_ref = f32[8128,128]{1,0:T(8,128)S(1)} custom-call(bf16[8016,4096]{1,0:T(8,128)(2,1)} %bitcast.9, bf16[96,4096]{1,0:T(8,128)(2,1)} %bitcast.11, f32[5,1002,1,128]{3,2,1,0:T(1,128)} %bitcast.10, s32[5,16]{1,0:T(8,128)} %bitcast.12), custom_call_target="tpu_custom_call" | custom-call | tf_op jit(solution)/shard_map/verify_exchange/pallas_call | solution.py:338
  78.2 1.7 %verify_finish.1 = (f32[5,1002,1,128]{3,2,1,0:T(1,128)}, f32[1002,1,128]{2,1,0:T(1,128)}, f32[1,5]{1,0:T(1,128)}, f32[1,1]{1,0:T(1,128)}) custom-call(f32[8128,128]{1,0:T(8,128)S(1)} %verify_exchange.1.pe_ref), custom_call_target="tpu_custom_call" | custom-call | tf_op jit(solution)/shard_map/verify_finish/pallas_call | solution.py:367

commit v7 on v6

--- a/solution.py
+++ b/solution.py
@@ -16,7 +16,7 @@
 MESH = pl.DeviceIdType.MESH
 
 
-GROUPS = (("F",), (1,), (1,), (2,), (4,), (8,), ("E", 8), (6,))
+GROUPS = (("F",), (1,), (1,), (2,), (4,), (8,), ("E", 9), (5,))
 HELD = 2
 LAST_SHARE = 4
 

time: 80 us -> 80 us (level)
  no operation moved by 1% of the time
where the time goes in v7:
time: 80 us; the launch traced here: 79.9 us
  Pallas kernels  79.2 us (99%)
    pallas_call x1, Pallas kernels, local_step(): pl.pallas_call(functools.partial(exchange_kernel, geo), name='verify_exch...  77.6 us
    pallas_call x1, Pallas kernels, local_step(): pl.pallas_call(functools.partial(finish_kernel, (total_rows, pitch, draft...  1.67 us

profile of v7, /device:TPU:21, one launch (start us, length us, event | category | flops | bytes accessed | tf_op | source)
XLA Modules:
  0.0 79.9 jit_solution(12378055058781838791)
XLA Ops:
  0.6 77.6 %verify_exchange.1.pe_ref = f32[8128,128]{1,0:T(8,128)S(1)} custom-call(bf16[8016,4096]{1,0:T(8,128)(2,1)} %bitcast.9, bf16[96,4096]{1,0:T(8,128)(2,1)} %bitcast.11, f32[5,1002,1,128]{3,2,1,0:T(1,128)} %bitcast.10, s32[5,16]{1,0:T(8,128)} %bitcast.12), custom_call_target="tpu_custom_call" | custom-call | tf_op jit(solution)/shard_map/verify_exchange/pallas_call | solution.py:338
  78.2 1.7 %verify_finish.1 = (f32[5,1002,1,128]{3,2,1,0:T(1,128)}, f32[1002,1,128]{2,1,0:T(1,128)}, f32[1,5]{1,0:T(1,128)}, f32[1,1]{1,0:T(1,128)}) custom-call(f32[8128,128]{1,0:T(8,128)S(1)} %verify_exchange.1.pe_ref), custom_call_target="tpu_custom_call" | custom-call | tf_op jit(solution)/shard_map/verify_finish/pallas_call | solution.py:367
